TPU v7x, 128 devices: a whole 4x4x4 slice. The times are simulated.
128 devices in a mesh: dp: 4 (over z), mp: 32 (over y, x, core).
Axes of the slice: x: 4, y: 4, z: 4, core: 2. Of those that a mesh axis runs over, the one named last changes fastest.
Arguments:
- latest_symbol_ids: int32 [256], P('dp'), may hold values from 0 to 65535
- lexicon_table: bfloat16 [65536, 4096], P('dp', 'mp'), may hold values from -40 to 40
- lexicon_layernorm_stretch: bfloat16 [4096], P('mp'), may hold values from 0.29882812 to 3
- lexicon_layernorm_shift: bfloat16 [4096], P('mp'), may hold values from -4 to 4
- recurrent_layernorm_stretch: bfloat16 [4096], P('mp'), may hold values from 0.25 to 1.75
- recurrent_layernorm_shift: bfloat16 [4096], P('mp'), may hold values from -3 to 3
- prior_recurrent_signal: bfloat16 [256, 4096], P('dp', 'mp'), may hold values from -6 to 6
- recurrent_lerp_coefs: bfloat16 [6, 4096], P(None, 'mp'), may hold values from 0 to 1
- forgetting_lowrank_first: bfloat16 [4096, 128], P('mp'), may hold values from -0.09375 to 0.09375
- forgetting_lowrank_second: bfloat16 [128, 4096], P(None, 'mp'), may hold values from -0.5 to 0.5
- forgetting_baseline: bfloat16 [4096], P('mp'), may hold values from -5 to 1
- learning_speed_lowrank_first: bfloat16 [4096, 128], P('mp'), may hold values from -0.09375 to 0.09375
- learning_speed_lowrank_second: bfloat16 [128, 4096], P(None, 'mp'), may hold values from -0.5 to 0.5
- learning_speed_baseline: bfloat16 [4096], P('mp'), may hold values from -2 to 2
- valve_lowrank_first: bfloat16 [4096, 480], P('mp'), may hold values from -0.09375 to 0.09375
- valve_lowrank_second: bfloat16 [480, 4096], P(None, 'mp'), may hold values from -0.25 to 0.25
- erasure_lookup_coefs: bfloat16 [4096], P('mp'), may hold values from 0.5 to 1.5
- lookup_speed_coefs: bfloat16 [4096], P('mp'), may hold values from 0.5 to 1.5
- present_reward_coefs: bfloat16 [4096], P('mp'), may hold values from -4 to 4
- acceptance_projection: bfloat16 [4096, 4096], P(None, 'mp'), may hold values from -0.09375 to 0.09375
- lookup_projection: bfloat16 [4096, 4096], P(None, 'mp'), may hold values from -0.09375 to 0.09375
- payload_projection: bfloat16 [4096, 4096], P(None, 'mp'), may hold values from -0.09375 to 0.09375
- memory_tensor: float32 [256, 64, 64, 64], P('dp', 'mp'), may hold values from -6 to 6
- cluster_layernorm_stretch: bfloat16 [4096], P('mp'), may hold values from 0.25 to 1.75
- cluster_layernorm_shift: bfloat16 [4096], P('mp'), may hold values from -3 to 3
- recurrent_result_proj: bfloat16 [4096, 4096], P('mp'), may hold values from -0.1875 to 0.1875
- feedforward_layernorm_stretch: bfloat16 [4096], P('mp'), may hold values from 0.25 to 1.75
- feedforward_layernorm_shift: bfloat16 [4096], P('mp'), may hold values from -3 to 3
- prior_feedforward_signal: bfloat16 [256, 4096], P('dp', 'mp'), may hold values from -6 to 6
- feedforward_lerp_coefs: bfloat16 [4096], P('mp'), may hold values from 0 to 1
- feedforward_lookup_proj: bfloat16 [4096, 16384], P(None, 'mp'), may hold values from -0.09375 to 0.09375
- feedforward_payload_proj: bfloat16 [16384, 4096], P('mp'), may hold values from -0.09375 to 0.09375
Outputs:
- hidden_out: float32 [256, 4096], P('dp', 'mp')
- refreshed_memory: float32 [256, 64, 64, 64], P('dp', 'mp')
- att_shift: bfloat16 [256, 4096], P('dp', 'mp')
- ffn_shift: bfloat16 [256, 4096], P('dp', 'mp')
- value_first: bfloat16 [256, 4096], P('dp', 'mp')
All inputs are finite; a program needn't handle non-finite values.
Results may differ from a plain program's by a relative error of at most 0.0095.
Values may be sent and summed in bfloat16 or wider, within the bound.
A program may use at most 128 MiB of HBM per device.

v0:
```python
import jax
import jax.numpy as jnp
from jax import lax
from jax.sharding import Mesh
from jax.sharding import PartitionSpec as P

FEATURE_SPAN = 4096
MP = ("mp_0", "mp_1", "mp_2")


def from_everyone(x, axis):
    peers = lax.axis_size(axis)
    return lax.all_to_all(jnp.broadcast_to(x[None], (peers, *x.shape)), axis, 0, 0, tiled=True)


def joined_along(tiles, dim):
    dims = list(tiles.shape[1:])
    dims[dim] *= tiles.shape[0]
    return jnp.moveaxis(tiles, 0, dim).reshape(dims)


def gathered_copies(x, axis, dim):
    tiles = from_everyone(x, axis)
    return joined_along(tiles, dim)


def in_blocks(x, dim, peers):
    dims = x.shape
    tiles = x.reshape(*dims[:dim], peers, dims[dim] // peers, *dims[dim + 1 :])
    return jnp.moveaxis(tiles, dim, 0)


def summed_on_arrival(x, axis, dim):
    peers = lax.axis_size(axis)
    tiles = lax.all_to_all(in_blocks(x, dim, peers), axis, 0, 0, tiled=True)
    return jnp.sum(tiles.astype(jnp.float32), axis=0)


def over_copies(x, axis):
    everything = from_everyone(x, axis)
    return jnp.sum(everything, axis=0)


def together(arrays, axis):
    vector, at, gathered = (jnp.concatenate([a.reshape(-1) for a in arrays]), 0, [])
    running = over_copies(vector, axis)
    for a in arrays:
        gathered.append(running[at : at + a.size].reshape(a.shape))
        at += a.size
    return tuple(gathered)


def sent_together(arrays, axis, dim, along):
    ends, at = ([], 0)
    for a in arrays[:-1]:
        at += a.shape[along]
        ends.append(at)
    both = jnp.concatenate(arrays, axis=along)
    return tuple(jnp.split(lax.all_gather(both, axis, axis=dim, tiled=True), ends, axis=along))


def summed_on_arrival_2(x, axis, dim):
    peers = lax.axis_size(axis)
    tiles = lax.all_to_all(in_blocks(x, dim, peers), axis, 0, 0, tiled=True)
    return jnp.sum(tiles, axis=0)


def filled_up(lines, peers):
    spare = -len(lines) % peers
    return jnp.pad(lines, [(0, spare)] + [(0, 0)] * (lines.ndim - 1))


def total_of(x, axes):
    own = summed_on_arrival_2(filled_up(x, lax.axis_size(axes)), axes, 0)
    whole = gathered_copies(own, axes, 0)
    return whole[: len(x)].reshape(x.shape)


def in_one(arrays, axis):
    vector, at, gathered = (jnp.concatenate([a.reshape(-1) for a in arrays]), 0, [])
    running = total_of(vector, axis)
    for a in arrays:
        gathered.append(running[at : at + a.size].reshape(a.shape))
        at += a.size
    return tuple(gathered)


def summed_rows(x, axes, dim):
    far, near = axes
    tiles = in_blocks(x, dim, lax.axis_size(far))
    nearer = summed_on_arrival_2(tiles, near, dim + 1)
    arrived = lax.all_to_all(nearer, far, split_axis=0, concat_axis=0, tiled=True)
    return arrived.sum(axis=0)


def gather_axes(x, axes, dim):
    far, near = axes
    tiles = from_everyone(from_everyone(x, far), near)
    return joined_along(tiles.swapaxes(0, 1).reshape(-1, *x.shape), dim)


def total_of_2(x, axes):
    lines = x.reshape(-1, x.shape[-1])
    own = summed_rows(filled_up(lines, lax.axis_size(axes[0]) * lax.axis_size(axes[1])), axes, 0)
    whole = gather_axes(own, axes, 0)
    return whole[: len(lines)].reshape(x.shape)


def matmul(left, right):
    return jnp.dot(left, right, preferred_element_type=jnp.float32)


def apply_norm(inputs, row_total, row_squares, norm_gain, norm_bias):
    row_mean = row_total / FEATURE_SPAN
    row_var = row_squares / FEATURE_SPAN - row_mean * row_mean
    scaled = (inputs - row_mean[:, None]) * lax.rsqrt(row_var + 1e-05)[:, None]
    return scaled * norm_gain.astype(jnp.float32) + norm_bias.astype(jnp.float32)


def recurrent_kernel(
    acceptance_vectors,
    raw_lookups,
    payload_vectors,
    forgetting_multiplier,
    learning_speed,
    result_valve,
    memory_tensor,
    erasure_lookup_coefs,
    lookup_speed_coefs,
    present_reward_coefs,
    cluster_layernorm_stretch,
    cluster_layernorm_shift,
):
    sequence_number = memory_tensor.shape[0]
    attention_parts = memory_tensor.shape[1]
    attention_span = memory_tensor.shape[2]
    regrouped_vectors = (sequence_number, attention_parts, attention_span)
    recept_heads = acceptance_vectors.reshape(regrouped_vectors)
    payload_each_part = payload_vectors.reshape(regrouped_vectors)
    decay_heads = forgetting_multiplier.reshape(regrouped_vectors)
    alpha_heads = learning_speed.reshape(regrouped_vectors)
    removal_key = (raw_lookups * erasure_lookup_coefs.astype(jnp.float32)).reshape(
        regrouped_vectors
    )
    removal_key = removal_key * lax.rsqrt(
        jnp.sum(removal_key * removal_key, axis=-1, keepdims=True) + 1e-06
    )
    stored_lookup_vectors = raw_lookups * (
        1.0 + (learning_speed - 1.0) * lookup_speed_coefs.astype(jnp.float32)
    )
    added_heads = stored_lookup_vectors.reshape(regrouped_vectors)
    removed = jnp.sum(memory_tensor * removal_key[:, :, None, :], axis=-1)
    new_state = (
        memory_tensor * decay_heads[:, :, None, :]
        - removed[:, :, :, None] * (removal_key * alpha_heads)[:, :, None, :]
        + payload_each_part[:, :, :, None] * added_heads[:, :, None, :]
    )
    readout = jnp.sum(new_state * recept_heads[:, :, None, :], axis=-1)
    head_mean = jnp.mean(readout, axis=-1, keepdims=True)
    head_var = jnp.mean(jnp.square(readout - head_mean), axis=-1, keepdims=True)
    standardized_signal = ((readout - head_mean) * lax.rsqrt(head_var + 0.00064)).reshape(
        sequence_number, attention_parts * attention_span
    )
    standardized_signal = standardized_signal * cluster_layernorm_stretch.astype(
        jnp.float32
    ) + cluster_layernorm_shift.astype(jnp.float32)
    present_reward = (
        jnp.sum(
            (
                acceptance_vectors
                * stored_lookup_vectors
                * present_reward_coefs.astype(jnp.float32)
            ).reshape(regrouped_vectors),
            axis=-1,
            keepdims=True,
        )
        * payload_each_part
    )
    valved_result = (
        standardized_signal
        + present_reward.reshape(sequence_number, attention_parts * attention_span)
    ) * result_valve
    return (valved_result.astype(jnp.bfloat16), new_state)


def per_device(
    latest_symbol_ids,
    lexicon_table,
    lexicon_layernorm_stretch,
    lexicon_layernorm_shift,
    recurrent_layernorm_stretch,
    recurrent_layernorm_shift,
    prior_recurrent_signal,
    recurrent_lerp_coefs,
    forgetting_lowrank_first,
    forgetting_lowrank_second,
    forgetting_baseline,
    learning_speed_lowrank_first,
    learning_speed_lowrank_second,
    learning_speed_baseline,
    valve_lowrank_first,
    valve_lowrank_second,
    erasure_lookup_coefs,
    lookup_speed_coefs,
    present_reward_coefs,
    acceptance_projection,
    lookup_projection,
    payload_projection,
    memory_tensor,
    cluster_layernorm_stretch,
    cluster_layernorm_shift,
    recurrent_result_proj,
    feedforward_layernorm_stretch,
    feedforward_layernorm_shift,
    prior_feedforward_signal,
    feedforward_lerp_coefs,
    feedforward_lookup_proj,
    feedforward_payload_proj,
):
    all_ids = gathered_copies(latest_symbol_ids, "dp", 0)
    vocab_rows = lexicon_table.shape[0]
    local_ids = all_ids - lax.axis_index("dp") * vocab_rows
    owned = (local_ids >= 0) & (local_ids < vocab_rows)
    picked = jnp.take(lexicon_table, jnp.clip(local_ids, 0, vocab_rows - 1), axis=0).astype(
        jnp.float32
    )
    picked = jnp.where(owned[:, None], picked, jnp.zeros_like(picked))
    emb_rows = summed_on_arrival(picked.astype(jnp.bfloat16), "dp", 0)
    gain_first = lexicon_layernorm_stretch.astype(jnp.float32)
    bias_first = lexicon_layernorm_shift.astype(jnp.float32)
    gain_square = gain_first * gain_first
    totals = together(
        (
            jnp.sum(emb_rows, axis=-1),
            jnp.sum(emb_rows * emb_rows, axis=-1),
            jnp.sum(emb_rows * gain_first, axis=-1),
            jnp.sum(emb_rows * emb_rows * gain_square, axis=-1),
            jnp.sum(emb_rows * gain_square, axis=-1),
            jnp.sum(emb_rows * (gain_first * bias_first), axis=-1),
            jnp.sum(gain_first),
            jnp.sum(gain_square),
            jnp.sum(gain_first * bias_first),
            jnp.sum(bias_first),
            jnp.sum(bias_first * bias_first),
        ),
        MP,
    )
    row_mean = totals[0] / FEATURE_SPAN
    inverse = lax.rsqrt(totals[1] / FEATURE_SPAN - row_mean * row_mean + 1e-05)
    residual = (emb_rows - row_mean[:, None]) * inverse[:, None] * gain_first + bias_first
    next_total = (totals[2] - row_mean * totals[6]) * inverse + totals[9]
    next_squares = (
        (totals[3] - 2.0 * row_mean * totals[4] + row_mean * row_mean * totals[7])
        * inverse
        * inverse
        + 2.0 * (totals[5] - row_mean * totals[8]) * inverse
        + totals[10]
    )
    att_in = apply_norm(
        residual, next_total, next_squares, recurrent_layernorm_stretch, recurrent_layernorm_shift
    ).astype(jnp.bfloat16)
    att_base = att_in.astype(jnp.float32)
    shift_delta = prior_recurrent_signal.astype(jnp.float32) - att_base
    mixed = [
        (att_base + shift_delta * recurrent_lerp_coefs[column].astype(jnp.float32)).astype(
            jnp.bfloat16
        )
        for column in range(6)
    ]
    recept_in, key_in, value_in, prior_full, gain_full, bias_full, mixing_full = sent_together(
        (
            mixed[0],
            mixed[2],
            mixed[3],
            prior_feedforward_signal,
            feedforward_layernorm_stretch[None, :],
            feedforward_layernorm_shift[None, :],
            feedforward_lerp_coefs[None, :],
        ),
        MP,
        1,
        0,
    )
    lows = in_one(
        (
            matmul(mixed[1], forgetting_lowrank_first),
            matmul(mixed[4], learning_speed_lowrank_first),
            matmul(mixed[5], valve_lowrank_first),
        ),
        MP,
    )
    acceptance_vectors = matmul(recept_in, acceptance_projection)
    raw_lookups = matmul(key_in, lookup_projection)
    payload_vectors = matmul(value_in, payload_projection)
    decay_low = jnp.tanh(lows[0]).astype(jnp.bfloat16)
    alpha_low = lows[1].astype(jnp.bfloat16)
    gate_low = jax.nn.sigmoid(lows[2]).astype(jnp.bfloat16)
    decay_log = (
        -jax.nn.softplus(
            -(
                forgetting_baseline.astype(jnp.float32)
                + matmul(decay_low, forgetting_lowrank_second)
            )
        )
        - 0.5
    )
    forgetting_multiplier = jnp.exp(-jnp.exp(decay_log))
    learning_speed = jax.nn.sigmoid(
        learning_speed_baseline.astype(jnp.float32)
        + matmul(alpha_low, learning_speed_lowrank_second)
    )
    result_valve = matmul(gate_low, valve_lowrank_second)
    recurrent_result, refreshed_memory = recurrent_kernel(
        acceptance_vectors,
        raw_lookups,
        payload_vectors,
        forgetting_multiplier,
        learning_speed,
        result_valve,
        memory_tensor,
        erasure_lookup_coefs,
        lookup_speed_coefs,
        present_reward_coefs,
        cluster_layernorm_stretch,
        cluster_layernorm_shift,
    )
    partial_out = matmul(recurrent_result, recurrent_result_proj)
    column_count = att_in.shape[1]
    start = lax.axis_index(MP) * column_count
    own_block = lax.dynamic_slice_in_dim(partial_out, start, column_count, 1) + residual
    partial_out = lax.dynamic_update_slice_in_dim(partial_out, own_block, start, 1)
    midway_full = total_of_2(partial_out, (("mp_0", "mp_1"), "mp_2"))
    ffn_full = apply_norm(
        midway_full,
        jnp.sum(midway_full, axis=-1),
        jnp.sum(midway_full * midway_full, axis=-1),
        gain_full[0],
        bias_full[0],
    ).astype(jnp.bfloat16)
    ffn_base = ffn_full.astype(jnp.float32)
    ffn_input = (
        ffn_base + (prior_full.astype(jnp.float32) - ffn_base) * mixing_full[0].astype(jnp.float32)
    ).astype(jnp.bfloat16)
    ffn_in = lax.dynamic_slice_in_dim(ffn_full, start, column_count, 1)
    midway = lax.dynamic_slice_in_dim(midway_full, start, column_count, 1)
    hidden = jnp.square(jax.nn.relu(matmul(ffn_input, feedforward_lookup_proj))).astype(
        jnp.bfloat16
    )
    hidden_out = midway + summed_on_arrival_2(matmul(hidden, feedforward_payload_proj), MP, 1)
    return (hidden_out, refreshed_memory, att_in, ffn_in, payload_vectors.astype(jnp.bfloat16))


def solution(mesh):
    torus = Mesh(mesh.devices.reshape(mesh.shape["dp"], 4, 4, 2), ("dp", "mp_0", "mp_1", "mp_2"))
    return jax.shard_map(
        per_device,
        mesh=torus,
        in_specs=(
            P("dp"),
            P("dp", MP),
            P(MP),
            P(MP),
            P(MP),
            P(MP),
            P("dp", MP),
            P(None, MP),
            P(MP, None),
            P(None, MP),
            P(MP),
            P(MP, None),
            P(None, MP),
            P(MP),
            P(MP, None),
            P(None, MP),
            P(MP),
            P(MP),
            P(MP),
            P(None, MP),
            P(None, MP),
            P(None, MP),
            P("dp", MP, None, None),
            P(MP),
            P(MP),
            P(MP, None),
            P(MP),
            P(MP),
            P("dp", MP),
            P(MP),
            P(None, MP),
            P(MP, None),
        ),
        out_specs=(P("dp", MP), P("dp", MP, None, None), P("dp", MP), P("dp", MP), P("dp", MP)),
        check_vma=False,
    )
```

profile of v0, /device:TPU:1, one launch (start us, length us, event | category | flops | bytes accessed | tf_op | source)
XLA Modules:
  0.0 213.7 jit_solution(4745499214020856221)
XLA Ops:
  7.2 1.4 broadcast_in_dim.36
  8.6 5.8 %all-to-all-start = ((s32[4,1,64]{2,1,0:T(1,128)}), s32[4,1,64]{2,1,0:T(1,128)S(1)}, u32[]{:S(2)}, u32[]{:S(2)}) async-start(s32[4,1,64]{2,1,0:T(1,128)} %broadcast_in_dim.36), calls=%async_computation | async-start | bytes 4096 | tf_op jit(solution)/shard_map/all_to_all | solution.py:13
  14.4 4.1 %all-to-all-done = s32[4,1,64]{2,1,0:T(1,128)S(1)} async-done(((s32[4,1,64]{2,1,0:T(1,128)}), s32[4,1,64]{2,1,0:T(1,128)S(1)}, u32[]{:S(2)}, u32[]{:S(2)}) %all-to-all-start) | async-done | bytes 1056 | tf_op jit(solution)/shard_map/all_to_all | solution.py:13
  19.8 3.5 %gather_fusion = bf16[256,128]{1,0:T(8,128)(2,1)S(1)} fusion(bf16[16384,128]{1,0:T(8,128)(2,1)} %param.33, s32[1024]{0:T(1024)S(1)} %pad_clamp_fusion), kind=kCustom, calls=%fused_computation | custom fusion | bytes 132096 | tf_op jit(solution)/shard_map/jit(_take)/gather | solution.py:224
  24.0 3.3 %all-to-all-start.1 = ((bf16[4,64,128]{2,1,0:T(8,128)(2,1)}), bf16[4,64,128]{2,1,0:T(8,128)(2,1)S(1)}, u32[]{:S(2)}, u32[]{:S(2)}) async-start(bf16[4,64,128]{2,1,0:T(8,128)(2,1)} %select_convert_fusion), calls=%async_computation.1 | async-start | bytes 131072 | tf_op jit(solution)/shard_map/all_to_all | solution.py:35
  27.3 1.4 multiply_reduce_fusion.11
  29.3 2.4 %all-to-all-done.1 = bf16[4,64,128]{2,1,0:T(8,128)(2,1)S(1)} async-done(((bf16[4,64,128]{2,1,0:T(8,128)(2,1)}), bf16[4,64,128]{2,1,0:T(8,128)(2,1)S(1)}, u32[]{:S(2)}, u32[]{:S(2)}) %all-to-all-start.1) | async-done | bytes 65568 | tf_op jit(solution)/shard_map/all_to_all | solution.py:35
  32.1 3.3 %concatenate.9 = f32[389]{0:T(512)S(1)} concatenate(f32[64]{0:T(128)S(1)} %get-tuple-element.9, f32[64]{0:T(128)S(1)} %get-tuple-element.15, f32[64]{0:T(128)S(1)} %get-tuple-element.14, f32[64]{0:T(128)S(1)} %get-tuple-element.12, f32[64]{0:T(128)S(1)} %get-tuple-element.11, f32[64]{0:T(128)S(1)} %get-tuple-element.13, f32[1]{0:T(128)} %bitcast.3, f32[1]{0:T(128)} %bitcast.4, ...), dimensions={0} | concatenate | bytes 3112 | tf_op jit(solution)/shard_map/concatenate | solution.py:45
  36.0 10.3 %all-to-all-start.2 = ((f32[32,1,389]{2,1,0:T(1,128)}), f32[32,1,389]{2,1,0:T(1,128)S(1)}, u32[]{:S(2)}, u32[]{:S(2)}) async-start(f32[32,1,389]{2,1,0:T(1,128)} %broadcast_in_dim.41), calls=%async_computation.2 | async-start | bytes 131072 | tf_op jit(solution)/shard_map/all_to_all | solution.py:13
  46.4 0.9 bitcast_convert_fusion.1
  49.3 4.4 %all-to-all-done.2 = f32[32,1,389]{2,1,0:T(1,128)S(1)} async-done(((f32[32,1,389]{2,1,0:T(1,128)}), f32[32,1,389]{2,1,0:T(1,128)S(1)}, u32[]{:S(2)}, u32[]{:S(2)}) %all-to-all-start.2) | async-done | bytes 49824 | tf_op jit(solution)/shard_map/all_to_all | solution.py:13
  55.7 2.1 add_rsqrt_fusion.3
  57.8 0.8 fusion.39
  59.5 4.4 %concatenate.11 = bf16[259,128]{1,0:T(8,128)(2,1)} concatenate(bf16[64,128]{1,0:T(8,128)(2,1)S(1)} %get-tuple-element.38, bf16[64,128]{1,0:T(8,128)(2,1)S(1)} %get-tuple-element.37, bf16[64,128]{1,0:T(8,128)(2,1)S(1)} %get-tuple-element.24, bf16[64,128]{1,0:T(8,128)(2,1)} %param.60, bf16[1,128]{1,0:T(2,128)(2,1)} %bitcast.82, bf16[1,128]{1,0:T(2,128)(2,1)} %bitcast.83, ...), dimensions={0} | concatenate | bytes 132608 | tf_op jit(solution)/shard_map/concatenate | solution.py:58
  63.9 1.1 fusion.51
  65.8 0.9 convolution_bitcast_fusion.1
  66.7 0.9 convolution_bitcast_fusion.2
  67.7 0.9 pad_maximum_fusion
  68.8 12.1 %all_to_all.57 = f32[32,1,1472]{2,1,0:T(1,128)S(1)} all-to-all(f32[32,1,1472]{2,1,0:T(1,128)S(1)} %all_to_all.39), channel_id=1, replica_groups=mesh['dp'=4,'mp_0'=4,'mp_1'=4,'mp_2'=2] {'mp_0','mp_1','mp_2'}, dimensions={0} | all-to-all | bytes 376832 | tf_op jit(solution)/shard_map/all_to_all | solution.py:64
  81.9 3.9 %all-to-all-start.4 = ((f32[32,1,1472]{2,1,0:T(1,128)}), f32[32,1,1472]{2,1,0:T(1,128)S(1)}, u32[]{:S(2)}, u32[]{:S(2)}) async-start(f32[32,1,1472]{2,1,0:T(1,128)} %broadcast_in_dim.42), calls=%async_computation.4 | async-start | bytes 393216 | tf_op jit(solution)/shard_map/all_to_all | solution.py:13
  85.8 1.2 convert_element_type.115
  87.0 1.2 convert_element_type.134
  88.2 1.2 convert_element_type.133
  89.4 1.2 convert_element_type.135
  90.6 1.2 convert_element_type.138
  91.7 1.2 convert_element_type.136
  93.0 1.2 convert_element_type.137
  95.7 1.0 fusion.44
  97.4 0.9 fusion.11
  98.5 6.4 %all-gather.2.cloned.1.call-done = bf16[259,4096]{1,0:T(8,128)(2,1)} async-done(((bf16[259,128]{1,0:T(8,128)(2,1)}), bf16[259,4096]{1,0:T(8,128)(2,1)}) %all-gather.2.cloned.1.call-update) | async-done | bytes 2121744 | tf_op jit(solution)/shard_map/all_gather | solution.py:59
  104.8 2.0 fusion.68
  106.9 1.7 fusion.25
  108.6 1.4 multiply_multiply_fusion
  111.1 19.8 %multiply_reduce_fusion.1 = (f32[64,2]{1,0:T(8,128)S(1)}, f32[64,2,64]{2,1,0:T(2,128)S(1)}, f32[64,2,64,64]{3,2,1,0:T(8,128)}) fusion(f32[64,2,64]{2,1,0:T(2,128)S(1)} %mul.497, f32[64,2,64]{2,1,0:T(2,128)S(1)} %mul.494, f32[64,2,64]{2,1,0:T(2,128)S(1)} %mul.489, f32[64,2,64]{2,1,0:T(2,128)S(1)} %get-tuple-element.20, f32[64,2,64,64]{3,2,1,0:T(8,128)} %param.54, ...), kind=kOutput, calls=%fused_computation.6 | output fusion | flops 4718527 | bytes 4424192 | tf_op jit(solution)/shard_map/mul | solution.py:155
  132.8 4.7 %all_to_all.58 = f32[2,16,2,4096]{3,2,1,0:T(2,128)S(1)} all-to-all(f32[2,16,2,4096]{3,2,1,0:T(2,128)S(1)} %bitcast.74), channel_id=1, replica_groups=mesh['dp'=4,'mp_0'=4,'mp_1'=4,'mp_2'=2] {'mp_2'}, dimensions={0} | all-to-all | bytes 2097152 | tf_op jit(solution)/shard_map/all_to_all | solution.py:64
  137.5 1.0 reduce_sum.245
  138.4 15.3 %all_to_all.59 = f32[16,2,4096]{2,1,0:T(2,128)S(1)} all-to-all(f32[16,2,4096]{2,1,0:T(2,128)S(1)} %reduce_sum.245), channel_id=1, replica_groups=mesh['dp'=4,'mp_0'=4,'mp_1'=4,'mp_2'=2] {'mp_0','mp_1'}, dimensions={0} | all-to-all | bytes 1048576 | tf_op jit(solution)/shard_map/all_to_all | solution.py:92
  153.9 1.0 broadcast_in_dim.46
  154.9 3.6 %all-to-all-start.7 = ((f32[16,2,4096]{2,1,0:T(2,128)}), f32[16,2,4096]{2,1,0:T(2,128)S(1)}, u32[]{:S(2)}, u32[]{:S(2)}) async-start(f32[16,2,4096]{2,1,0:T(2,128)} %broadcast_in_dim.46), calls=%async_computation.7 | async-start | bytes 1048576 | tf_op jit(solution)/shard_map/all_to_all | solution.py:13
  158.4 1.0 slice_convert_fusion.2
  159.4 9.1 %all-to-all-done.7 = f32[16,2,4096]{2,1,0:T(2,128)S(1)} async-done(((f32[16,2,4096]{2,1,0:T(2,128)}), f32[16,2,4096]{2,1,0:T(2,128)S(1)}, u32[]{:S(2)}, u32[]{:S(2)}) %all-to-all-start.7) | async-done | bytes 524320 | tf_op jit(solution)/shard_map/all_to_all | solution.py:13
  169.0 6.6 %all_to_all.60 = f32[2,16,2,4096]{3,2,1,0:T(2,128)S(1)} all-to-all(f32[2,16,2,4096]{3,2,1,0:T(2,128)S(1)} %broadcast_in_dim.47), channel_id=1, replica_groups=mesh['dp'=4,'mp_0'=4,'mp_1'=4,'mp_2'=2] {'mp_2'}, dimensions={0} | all-to-all | bytes 2097152 | tf_op jit(solution)/shard_map/all_to_all | solution.py:13
  177.5 1.0 add_convert_fusion
  178.6 5.3 %convolution_bitcast_fusion = f32[8,32,8,128]{3,2,1,0:T(8,128)S(1)} fusion(bf16[512,4096]{1,0:T(8,128)(2,1)} %param.63, bf16[4096,512]{1,0:T(8,128)(2,1)} %param.62, bf16[64,4096]{1,0:T(8,128)(2,1)} %add_convert_fusion, bf16[259,4096]{1,0:T(8,128)(2,1)} %all-gather.2.cloned.1.call-done, f32[4096]{0:T(1024)S(1)} %bitcast.76), kind=kOutput, calls=%fused_computation.9 | convolution fusion | flops 538542080 | bytes 10502144 | tf_op jit(solution)/shard_map/dot_general | solution.py:110
  183.9 1.1 copy.94
  185.0 4.0 %all-to-all-start.9 = ((f32[32,64,128]{2,1,0:T(8,128)}), f32[32,64,128]{2,1,0:T(8,128)S(1)}, u32[]{:S(2)}, u32[]{:S(2)}) async-start(f32[32,64,128]{2,1,0:T(8,128)} %bitcast.73), calls=%async_computation.9 | async-start | bytes 2097152 | tf_op jit(solution)/shard_map/all_to_all | solution.py:64
  189.0 1.3 constant_dynamic-slice_fusion
  190.3 15.8 %all-to-all-done.9 = f32[32,64,128]{2,1,0:T(8,128)S(1)} async-done(((f32[32,64,128]{2,1,0:T(8,128)}), f32[32,64,128]{2,1,0:T(8,128)S(1)}, u32[]{:S(2)}, u32[]{:S(2)}) %all-to-all-start.9) | async-done | bytes 1048608 | tf_op jit(solution)/shard_map/all_to_all | solution.py:64
  (101 shorter events, 17.6 us)
Async XLA Ops:
  7.2 124.3 %copy-start = (bf16[128,4096]{1,0:T(8,128)(2,1)S(1)}, bf16[128,4096]{1,0:T(8,128)(2,1)}, u32[]{:S(2)}) copy-start(bf16[128,4096]{1,0:T(8,128)(2,1)} %param.57) | copy-start | bytes 3145732
  7.2 97.6 %copy-start.2 = (bf16[4096,128]{1,0:T(8,128)(2,1)S(1)}, bf16[4096,128]{1,0:T(8,128)(2,1)}, u32[]{:S(2)}) copy-start(bf16[4096,128]{1,0:T(8,128)(2,1)} %param.53) | copy-start | bytes 3145732
  8.6 9.9 %all-to-all-start = ((s32[4,1,64]{2,1,0:T(1,128)}), s32[4,1,64]{2,1,0:T(1,128)S(1)}, u32[]{:S(2)}, u32[]{:S(2)}) async-start(s32[4,1,64]{2,1,0:T(1,128)} %broadcast_in_dim.36), calls=%async_computation | async-start | bytes 4096 | tf_op jit(solution)/shard_map/all_to_all | solution.py:13
  24.0 7.7 %all-to-all-start.1 = ((bf16[4,64,128]{2,1,0:T(8,128)(2,1)}), bf16[4,64,128]{2,1,0:T(8,128)(2,1)S(1)}, u32[]{:S(2)}, u32[]{:S(2)}) async-start(bf16[4,64,128]{2,1,0:T(8,128)(2,1)} %select_convert_fusion), calls=%async_computation.1 | async-start | bytes 131072 | tf_op jit(solution)/shard_map/all_to_all | solution.py:35
  29.3 37.4 %copy-start.8 = (f32[128]{0:T(128)}, f32[128]{0:T(128)S(1)}, u32[]{:S(2)}) copy-start(f32[128]{0:T(128)S(1)} %convert_element_type.119) | copy-start | bytes 1540
  31.9 35.8 %copy-start.3 = (f32[64,128]{1,0:T(8,128)}, f32[64,128]{1,0:T(8,128)S(1)}, u32[]{:S(2)}) copy-start(f32[64,128]{1,0:T(8,128)S(1)} %get-tuple-element.10) | copy-start | bytes 98308
  36.0 17.7 %all-to-all-start.2 = ((f32[32,1,389]{2,1,0:T(1,128)}), f32[32,1,389]{2,1,0:T(1,128)S(1)}, u32[]{:S(2)}, u32[]{:S(2)}) async-start(f32[32,1,389]{2,1,0:T(1,128)} %broadcast_in_dim.41), calls=%async_computation.2 | async-start | bytes 131072 | tf_op jit(solution)/shard_map/all_to_all | solution.py:13
  46.4 58.5 %all-gather.2.cloned.1.call-start = ((), (), s32[]{:S(2)}) async-start(), calls=%async_computation.10 | async-start | bytes 2230272 | tf_op jit(solution)/shard_map/all_gather | solution.py:59
  48.0 18.8 %copy-start.14 = (f32[128]{0:T(128)}, f32[128]{0:T(128)S(1)}, u32[]{:S(2)}) copy-start(f32[128]{0:T(128)S(1)} %convert_element_type.120) | copy-start | bytes 1540
  57.8 0.9 copy-start.10
  57.8 0.9 copy-start.12
  58.6 51.4 %copy-start.5 = (bf16[64,128]{1,0:T(8,128)(2,1)}, bf16[64,128]{1,0:T(8,128)(2,1)S(1)}, u32[]{:S(2)}) copy-start(bf16[64,128]{1,0:T(8,128)(2,1)S(1)} %get-tuple-element.25) | copy-start | bytes 49156
  58.6 50.0 %copy-start.1 = (bf16[4096,128]{1,0:T(8,128)(2,1)S(1)}, bf16[4096,128]{1,0:T(8,128)(2,1)}, u32[]{:S(2)}) copy-start(bf16[4096,128]{1,0:T(8,128)(2,1)} %param.51) | copy-start | bytes 3145732
  81.9 12.3 %all-to-all-start.4 = ((f32[32,1,1472]{2,1,0:T(1,128)}), f32[32,1,1472]{2,1,0:T(1,128)S(1)}, u32[]{:S(2)}, u32[]{:S(2)}) async-start(f32[32,1,1472]{2,1,0:T(1,128)} %broadcast_in_dim.42), calls=%async_computation.4 | async-start | bytes 393216 | tf_op jit(solution)/shard_map/all_to_all | solution.py:13
  106.8 4.2 %copy-start.7 = (f32[64,2,64]{2,1,0:T(2,128)S(1)}, f32[64,2,64]{2,1,0:T(2,128)}, u32[]{:S(2)}) copy-start(f32[64,2,64]{2,1,0:T(2,128)} %mul.463) | copy-start | bytes 98308
  111.0 20.5 %copy-start.6 = (bf16[480,128]{1,0:T(8,128)(2,1)S(1)}, bf16[480,128]{1,0:T(8,128)(2,1)}, u32[]{:S(2)}) copy-start(bf16[480,128]{1,0:T(8,128)(2,1)} %param.47) | copy-start | bytes 368644
  111.0 20.5 %copy-start.16 = (f32[128]{0:T(128)S(1)}, f32[128]{0:T(128)}, u32[]{:S(2)}) copy-start(f32[128]{0:T(128)} %convert_element_type.136) | copy-start | bytes 1540
  111.0 20.5 %copy-start.17 = (f32[128]{0:T(128)S(1)}, f32[128]{0:T(128)}, u32[]{:S(2)}) copy-start(f32[128]{0:T(128)} %convert_element_type.137) | copy-start | bytes 1540
  111.0 20.9 %copy-start.4 = (f32[64,128]{1,0:T(8,128)S(1)}, f32[64,128]{1,0:T(8,128)}, u32[]{:S(2)}) copy-start(f32[64,128]{1,0:T(8,128)} %copy-done.3) | copy-start | bytes 98308
  111.0 20.9 %copy-start.9 = (f32[128]{0:T(128)S(1)}, f32[128]{0:T(128)}, u32[]{:S(2)}) copy-start(f32[128]{0:T(128)} %copy-done.8) | copy-start | bytes 1540
  111.0 20.9 %copy-start.11 = (f32[64]{0:T(128)S(1)}, f32[64]{0:T(128)}, u32[]{:S(2)}) copy-start(f32[64]{0:T(128)} %copy-done.10) | copy-start | bytes 772
  111.1 20.9 %copy-start.13 = (f32[64]{0:T(128)S(1)}, f32[64]{0:T(128)}, u32[]{:S(2)}) copy-start(f32[64]{0:T(128)} %copy-done.12) | copy-start | bytes 772
  111.1 20.9 %copy-start.15 = (f32[128]{0:T(128)S(1)}, f32[128]{0:T(128)}, u32[]{:S(2)}) copy-start(f32[128]{0:T(128)} %copy-done.14) | copy-start | bytes 1540
  154.9 13.7 %all-to-all-start.7 = ((f32[16,2,4096]{2,1,0:T(2,128)}), f32[16,2,4096]{2,1,0:T(2,128)S(1)}, u32[]{:S(2)}, u32[]{:S(2)}) async-start(f32[16,2,4096]{2,1,0:T(2,128)} %broadcast_in_dim.46), calls=%async_computation.7 | async-start | bytes 1048576 | tf_op jit(solution)/shard_map/all_to_all | solution.py:13
  185.0 21.1 %all-to-all-start.9 = ((f32[32,64,128]{2,1,0:T(8,128)}), f32[32,64,128]{2,1,0:T(8,128)S(1)}, u32[]{:S(2)}, u32[]{:S(2)}) async-start(f32[32,64,128]{2,1,0:T(8,128)} %bitcast.73), calls=%async_computation.9 | async-start | bytes 2097152 | tf_op jit(solution)/shard_map/all_to_all | solution.py:64
Sparse Core Ops, SparseCore 0:
  64.1 40.7 all-gather.1
where the time goes:
time: 215 us; the launch traced here: 214 us
  other arithmetic  45.8 us (21%)
  waiting for transfers between devices  42.1 us (20%)
  blocking collectives  38.7 us (18%)
  starting transfers between devices  30.9 us (14%)
  local copies, waits for them, and re-layouts  24.6 us (11%)
  between operations  15.9 us (7%)
  matrix products  15.6 us (7%)
    all_to_all x4, starting transfers between devices, from_everyone(): lax.all_to_all(jnp.broadcast_to(x[None], (peers, *x.shape)), axis, 0, 0,...  23.6 us
    mul x1, other arithmetic, recurrent_kernel(): removed[:, :, :, None] * (removal_key * alpha_heads)[:, :, None, :]  19.8 us
    all_to_all x4, waiting for transfers between devices, from_everyone(): lax.all_to_all(jnp.broadcast_to(x[None], (peers, *x.shape)), axis, 0, 0,...  17.5 us
    all_to_all x2, blocking collectives, summed_on_arrival_2(): tiles = lax.all_to_all(in_blocks(x, dim, peers), axis, 0, 0, tiled=True)  16.8 us
    all_to_all x1, waiting for transfers between devices, summed_on_arrival_2(): tiles = lax.all_to_all(in_blocks(x, dim, peers), axis, 0, 0, tiled=True)  15.8 us
    dot_general x10, matrix products, matmul(): return jnp.dot(left, right, preferred_element_type=jnp.float32)  15.6 us
    all_to_all x1, blocking collectives, summed_rows(): lax.all_to_all(nearer, far, split_axis=0, concat_axis=0, tiled=True)  15.3 us
    all_to_all x1, blocking collectives, from_everyone(): lax.all_to_all(jnp.broadcast_to(x[None], (peers, *x.shape)), axis, 0, 0,...  6.62 us
  transfers between devices with their start and end apart: 7, of which 6 were waited for; matrix products, arithmetic and copies ran while one was open for 12% of the time, Pallas kernels for 0%

commit v1 on v0

v1 whole, which is shorter than its diff:
```python
import jax
import jax.numpy as jnp
from jax import lax
from jax.experimental import pallas as pl
from jax.experimental.pallas import tpu as pltpu
from jax.sharding import PartitionSpec as P

MESH = pl.DeviceIdType.MESH
F32 = jnp.float32
BF16 = jnp.bfloat16
N = 4096
NQ = 16
NM = 32
ND = 4
LOW = 23
V_RK, V_DR, V_D, V_RKA, V_W, V_V, V_REM = range(7)
E_HALF = 0.6065306597126334


def whole_step(
    ids, table, prior_rec, lerp, wd1, wd2, wa1, wa2, wg1, wg2, wr, wk, wv, state, wo, prior_ffn, wup, wdn,
    g1, b1, g2, b2, g3, b3, lerp_ffn, fbase, abase, erase, lcoef, reward, clg, clb,
    out_h, out_s, out_att, out_ffn, out_v,
    idv, ids_s, tab, prm, lerp_v, wd1_v, wd2_v, wa1_v, wa2_v, wg1_v, wg2_v, wr_v, wk_v, wv_v, s_v,
    wop, wup_v, wdp, rows_s, rows_r, abuf, ebuf, fbuf, mbuf, wts, wt, mx, res, lt, vec, rowb, ap, zf, zs, zr, zs2, zr2, hp,
    ov_h, ov_att, ov_ffn, ov_v,
    ld, zsem, asem, esem, fsem, msem, wsem, wrecv, ltsend, ltrecv, psem, z1sem, z2sem, hsem, osem,
):
    d = lax.axis_index("dp")
    me = lax.axis_index("mp")
    q = me // 2
    c = me % 2
    mate = me + 1 - 2 * c

    def remote(src, dst, ssem, rsem, dev):
        return pltpu.make_async_remote_copy(
            src_ref=src, dst_ref=dst, send_sem=ssem, recv_sem=rsem, device_id=dev, device_id_type=MESH
        )

    def lanes(i):
        return pl.ds(pl.multiple_of(i * 128, 128), 128)

    loads = []

    def load(src, dst):
        k = pltpu.make_async_copy(src, dst, ld.at[len(loads)])
        k.start()
        loads.append(k)
        return k

    l_ids = load(ids, idv.at[d])
    l_prm = [
        load(p, prm.at[i])
        for i, p in enumerate((g1, b1, g2, b2, g3, b3, lerp_ffn, fbase, abase, erase, lcoef, reward, clg, clb))
    ]
    l_prm.append(load(lerp, lerp_v))
    l_prior = load(prior_rec, abuf.at[c, q, pl.ds(16, 64), :])
    l_low = [load(wd1, wd1_v), load(wa1, wa1_v), load(wg1, wg1_v)]
    l_tab = load(table, tab)
    l_rkv = [load(wk, wk_v), load(wv, wv_v), load(wr, wr_v)]
    l_s = load(state, s_v)
    l_low2 = [load(wd2, wd2_v), load(wa2, wa2_v), load(wg2, wg2_v)]
    l_priorf = load(prior_ffn, fbuf.at[c, q])

    barrier = pltpu.get_barrier_semaphore()

    @pl.loop(1, ND)
    def _(i):
        pl.semaphore_signal(barrier, inc=1, device_id=((d + i) % ND, me), device_id_type=MESH)

    @pl.loop(1, NM)
    def _(i):
        pl.semaphore_signal(barrier, inc=1, device_id=(d, (me + i) % NM), device_id_type=MESH)

    for k in l_prm:
        k.wait()
    par = lambda i: prm[i].astype(F32)
    lerp_own = lerp_v[...].astype(F32)
    packed = jnp.concatenate(
        [par(0), par(1), par(2), par(3), lerp_own, par(4), par(5), par(6), jnp.zeros((3, 128), F32)], axis=0
    )
    abuf[c, q, 0:16, :] = packed.astype(BF16)
    for k in l_low:
        k.wait()
    wts[0:128, :] = jnp.transpose(wd1_v[...].astype(F32)).astype(BF16)
    wts[128:256, :] = jnp.transpose(wa1_v[...].astype(F32)).astype(BF16)
    for t in range(3):
        wts[256 + 128 * t : 384 + 128 * t, :] = jnp.transpose(
            wg1_v[:, 128 * t : 128 * t + 128].astype(F32)
        ).astype(BF16)
    wts[640:736, :] = jnp.transpose(wg1_v[:, 384:480].astype(F32)).astype(BF16)
    l_ids.wait()
    l_prior.wait()

    pl.semaphore_wait(barrier, ND - 1 + NM - 1)

    @pl.loop(1, ND)
    def _(i):
        remote(idv.at[d], idv.at[d], zsem.at[0], zsem.at[1], ((d + i) % ND, me)).start()

    def gather_start(buf, sem):
        @pl.loop(1, NQ)
        def _(i):
            remote(buf.at[c, q], buf.at[c, q], sem.at[0], sem.at[1], (d, 2 * ((q + i) % NQ) + c)).start()

    def gather_finish(buf, sem):
        part = buf.at[0, pl.ds(0, NQ - 1)]
        remote(part, part, sem.at[0], sem.at[1], (d, mate)).wait_recv()
        k = remote(buf.at[c], buf.at[c], sem.at[2], sem.at[3], (d, mate))
        k.start()
        return k

    def gather_sent(buf, sem):
        part = buf.at[0, pl.ds(0, NQ - 1)]
        remote(part, part, sem.at[0], sem.at[1], (d, mate)).wait_send()

    gather_start(abuf, asem)

    @pl.loop(0, LOW)
    def _(j):
        @pl.when(j != me)
        def _():
            remote(
                wts.at[pl.ds(pl.multiple_of(j * 32, 32), 32), :], wt.at[:, lanes(me)], wsem.at[j], wrecv, (d, j)
            ).start()

    @pl.when(me < LOW)
    def _():
        wt[:, lanes(me)] = wts[pl.ds(pl.multiple_of(me * 32, 32), 32), :]

    own_w = []
    for t in range(NQ):
        own_w.append(
            (
                pltpu.make_async_copy(
                    wo.at[:, lanes(2 * t + c)],
                    wop.at[pl.ds(pl.multiple_of(c * 128, 128), 128), pl.ds(t * 128, 128)],
                    psem.at[0],
                ),
                remote(
                    wo.at[:, lanes(2 * t + 1 - c)],
                    wop.at[pl.ds(pl.multiple_of(c * 128, 128), 128), pl.ds(t * 128, 128)],
                    psem.at[1],
                    psem.at[2],
                    (d, mate),
                ),
                pltpu.make_async_copy(
                    wdn.at[:, lanes(2 * t + c)],
                    wdp.at[pl.ds(pl.multiple_of(c * 512, 512), 512), pl.ds(t * 128, 128)],
                    psem.at[3],
                ),
                remote(
                    wdn.at[:, lanes(2 * t + 1 - c)],
                    wdp.at[pl.ds(pl.multiple_of(c * 512, 512), 512), pl.ds(t * 128, 128)],
                    psem.at[4],
                    psem.at[5],
                    (d, mate),
                ),
            )
        )
    for k in own_w:
        k[0].start()
        k[1].start()
    l_up = load(wup, wup_v)
    for k in own_w:
        k[2].start()
        k[3].start()

    part = idv.at[pl.ds(0, ND - 1)]
    remote(part, part, zsem.at[0], zsem.at[1], (d, mate)).wait_recv()
    k = pltpu.make_async_copy(idv, ids_s, ld.at[len(loads)])
    k.start()
    l_tab.wait()
    k.wait()
    base = d * tab.shape[0] * 8
    sub8 = lax.broadcasted_iota(jnp.int32, (8, 128), 0)

    for s in range(ND):
        @pl.loop(0, 8)
        def _(g, s=s):
            block = jnp.zeros((8, 128), F32)
            for u in range(8):
                at = ids_s[s, 0, g * 8 + u] - base
                inside = jnp.logical_and(at >= 0, at < tab.shape[0] * 8)
                at = jnp.where(inside, at, 0)
                eight = tab[at // 8].astype(F32)
                want = jnp.where(inside, at % 8, 8)
                row = jnp.sum(jnp.where(sub8 == want, eight, 0.0), axis=0, keepdims=True)
                block = jnp.where(sub8 == u, row, block)
            rowb[0, pl.ds(pl.multiple_of(g * 8, 8), 8), :] = block

        rows_s[s] = rowb[0].astype(BF16)

        @pl.when(d != s)
        def _(s=s):
            remote(rows_s.at[s], rows_r.at[d], zsem.at[2], zsem.at[3], (s, me)).start()

    for s in range(ND):
        @pl.when(d == s)
        def _(s=s):
            rows_r[s] = rows_s[s]

    a_fwd = gather_finish(abuf, asem)

    part = rows_r.at[pl.ds(0, ND - 1)]
    remote(part, part, zsem.at[2], zsem.at[3], (d, mate)).wait_recv()
    found = rows_r[0].astype(F32)
    for s in range(1, ND):
        found = found + rows_r[s].astype(F32)
    ebuf[c, q] = found.astype(BF16)
    gather_start(ebuf, esem)
    l_priorf.wait()
    gather_start(fbuf, fsem)
    e_fwd = gather_finish(ebuf, esem)
    a_fwd.wait_recv()
    e_fwd.wait_recv()

    def params(cc, t):
        return abuf[cc, t, 0:16, :].astype(F32)

    zero = jnp.zeros((64, 128), F32)

    def over_blocks(body, init):
        def step(t, acc):
            for cc in (0, 1):
                acc = body(cc, t, acc)
            return acc

        return lax.fori_loop(0, NQ, step, init)

    def rowsum(x):
        return jnp.sum(x, axis=-1, keepdims=True)

    mean1 = rowsum(over_blocks(lambda cc, t, acc: acc + ebuf[cc, t].astype(F32), zero)) / N
    inv1 = lax.rsqrt(
        rowsum(over_blocks(lambda cc, t, acc: acc + jnp.square(ebuf[cc, t].astype(F32) - mean1), zero)) / N + 1e-05
    )

    def first_norm(cc, t, acc):
        p = params(cc, t)
        r = (ebuf[cc, t].astype(F32) - mean1) * inv1 * p[0:1] + p[1:2]
        res[cc, t] = r
        return acc + r

    mean2 = rowsum(over_blocks(first_norm, zero)) / N
    inv2 = lax.rsqrt(rowsum(over_blocks(lambda cc, t, acc: acc + jnp.square(res[cc, t] - mean2), zero)) / N + 1e-05)

    def mixing(cc, t, acc):
        p = params(cc, t)
        att = ((res[cc, t] - mean2) * inv2 * p[2:3] + p[3:4]).astype(BF16).astype(F32)
        delta = abuf[cc, t, 16:80, :].astype(F32) - att
        low = jnp.where(me < 4, p[5:6], jnp.where(me < 8, p[8:9], p[9:10]))
        at = lanes(2 * t + cc)
        mx[0, :, at] = (att + delta * low).astype(BF16)
        mx[1, :, at] = (att + delta * p[6:7]).astype(BF16)
        mx[2, :, at] = (att + delta * p[7:8]).astype(BF16)
        mx[3, :, at] = (att + delta * p[4:5]).astype(BF16)
        return acc

    over_blocks(mixing, 0)
    own_res = res[c, q]
    ov_att[...] = ((own_res - mean2) * inv2 * par(2) + par(3)).astype(BF16)
    outs = [pltpu.make_async_copy(ov_att, out_att, osem.at[0])]
    outs[0].start()

    @pl.when(me < LOW)
    def _():
        got = wt.at[:, pl.ds(0, (NM - 1) * 128)]
        remote(got, got, wsem.at[0], wrecv, (d, mate)).wait_recv()
        low = lax.dot_general(wt[...], mx[0], (((1,), (1,)), ((), ())), preferred_element_type=F32)
        low = jnp.where(me < 4, jnp.tanh(low), jnp.where(me < 8, low, jax.nn.sigmoid(low)))
        lt[me] = low.astype(BF16)

        @pl.loop(1, NM)
        def _(i):
            remote(lt.at[me], lt.at[me], ltsend, ltrecv.at[me], (d, (me + i) % NM)).start()

    def head_rows(i, x):
        vec[i, 0] = x
        vec[i, 1] = pltpu.roll(x, 64, axis=1)

    left = lax.broadcasted_iota(jnp.int32, (64, 128), 1) < 64
    eye = lax.broadcasted_iota(jnp.int32, (64, 64), 0) == lax.broadcasted_iota(jnp.int32, (64, 64), 1)

    def headsum(x):
        return jnp.where(left, rowsum(jnp.where(left, x, 0.0)), rowsum(jnp.where(left, 0.0, x)))

    def projected(i, w, k):
        k.wait()
        return jnp.dot(mx[i], w[...], preferred_element_type=F32)

    def state_times(i):
        @pl.loop(0, 64)
        def _(b):
            for h in (0, 1):
                col = rowsum(s_v[b, h] * vec[i, h, pl.ds(b, 1), 0:64])
                rowb[h, pl.ds(b, 1), 0:64] = jnp.sum(jnp.where(eye, col, 0.0), axis=0, keepdims=True)

        return jnp.where(left, rowb[0], pltpu.roll(rowb[1], 64, axis=1))

    keys = projected(1, wk_v, l_rkv[0])
    removal = keys * par(9)
    removal = removal * lax.rsqrt(headsum(removal * removal) + 1e-06)
    values = projected(2, wv_v, l_rkv[1])
    recept = projected(3, wr_v, l_rkv[2])
    ov_v[...] = values.astype(BF16)
    outs.append(pltpu.make_async_copy(ov_v, out_v, osem.at[1]))
    outs[1].start()
    head_rows(V_RK, removal)
    head_rows(V_V, values)
    rowb[0] = zero
    rowb[1] = zero
    l_s.wait()
    removed = state_times(V_RK)
    head_rows(V_REM, removed)

    for k in l_low2:
        k.wait()

    @pl.loop(0, LOW)
    def _(j):
        @pl.when(j != me)
        def _():
            remote(lt.at[j], lt.at[j], ltsend, ltrecv.at[j], (d, mate)).wait_recv()

    def second(lo, hi, w):
        low = lt[lo:hi].astype(F32).reshape((hi - lo) * 32, 64)
        return jnp.dot(jnp.transpose(low).astype(BF16), w[...], preferred_element_type=F32)

    decay = jnp.exp(-E_HALF * jax.nn.sigmoid(par(7) + second(0, 4, wd2_v)))
    alpha = jax.nn.sigmoid(par(8) + second(4, 8, wa2_v))
    gate = second(8, LOW, wg2_v)
    written = keys * (1.0 + (alpha - 1.0) * par(10))
    rka = removal * alpha
    head_rows(V_D, decay)
    head_rows(V_RKA, rka)
    head_rows(V_W, written)
    head_rows(V_DR, decay * recept)
    readout = (
        state_times(V_DR) - removed * headsum(rka * recept) + values * headsum(written * recept)
    )
    centered = readout - headsum(readout) / 64
    normed = centered * lax.rsqrt(headsum(centered * centered) / 64 + 0.00064) * par(12) + par(13)
    bonus = headsum(recept * written * par(11)) * values
    ap[c] = ((normed + bonus) * gate).astype(BF16)
    k = remote(ap.at[c], ap.at[c], hsem.at[0], hsem.at[1], (d, mate))
    k.start()

    wo_own = wop.at[pl.ds(0, 128), :]
    pltpu.make_async_copy(wo_own, wo_own, psem.at[0]).wait()
    remote(wo_own, wo_own, psem.at[1], psem.at[2], (d, mate)).wait_recv()
    k.wait()

    def scatter(pair, w, send, recv, sem):
        @pl.loop(0, NQ // 2)
        def _(i):
            t = (i + q // 2) % (NQ // 2)
            y = jnp.dot(
                pair, w[:, pl.ds(pl.multiple_of(t * 256, 256), 256)], preferred_element_type=F32
            )
            for u in (0, 1):
                to = 2 * t + u
                block = y[:, 128 * u : 128 * u + 128]
                send[to] = block.astype(BF16)

                @pl.when(to != q)
                def _(to=to):
                    remote(send.at[to], recv.at[q], sem.at[0], sem.at[1], (d, 2 * to + c)).start()

                @pl.when(to == q)
                def _(block=block):
                    zf[...] = block
                    recv[q] = jnp.zeros((64, 128), BF16)

    def arrived(recv, sem):
        part = recv.at[pl.ds(0, NQ - 1)]
        remote(part, part, sem.at[0], sem.at[1], (d, mate)).wait_recv()
        total = zf[...]
        for t in range(NQ):
            total = total + recv[t].astype(F32)
        return total

    scatter(jnp.concatenate([ap[0], ap[1]], axis=1), wop, zs, zr, z1sem)

    @pl.loop(0, 64)
    def _(b):
        for h in (0, 1):
            row = lambda i: vec[i, h, pl.ds(b, 1), 0:64]
            gone = rowsum(jnp.where(eye, row(V_REM), 0.0))
            val = rowsum(jnp.where(eye, row(V_V), 0.0))
            s_v[b, h] = s_v[b, h] * row(V_D) - gone * row(V_RKA) + val * row(V_W)

    outs.append(pltpu.make_async_copy(s_v, out_s, osem.at[2]))
    outs[2].start()

    f_fwd = gather_finish(fbuf, fsem)
    midway = own_res + arrived(zr, z1sem)
    mbuf[c, q] = midway.astype(BF16)
    gather_start(mbuf, msem)
    f_fwd.wait_recv()
    m_fwd = gather_finish(mbuf, msem)
    m_fwd.wait_recv()

    mean3 = rowsum(over_blocks(lambda cc, t, acc: acc + mbuf[cc, t].astype(F32), zero)) / N
    inv3 = lax.rsqrt(
        rowsum(over_blocks(lambda cc, t, acc: acc + jnp.square(mbuf[cc, t].astype(F32) - mean3), zero)) / N + 1e-05
    )

    def ffn_mixing(cc, t, acc):
        p = params(cc, t)
        base = ((mbuf[cc, t].astype(F32) - mean3) * inv3 * p[10:11] + p[11:12]).astype(BF16).astype(F32)
        mx[0, :, lanes(2 * t + cc)] = (base + (fbuf[cc, t].astype(F32) - base) * p[12:13]).astype(BF16)
        return acc

    over_blocks(ffn_mixing, 0)
    l_up.wait()
    up = jnp.dot(mx[0], wup_v[...], preferred_element_type=F32)
    hp[c] = jnp.square(jnp.maximum(up, 0.0)).astype(BF16)
    k = remote(hp.at[c], hp.at[c], hsem.at[2], hsem.at[3], (d, mate))
    k.start()
    ov_ffn[...] = ((midway - mean3) * inv3 * par(4) + par(5)).astype(BF16)
    outs.append(pltpu.make_async_copy(ov_ffn, out_ffn, osem.at[3]))
    outs[3].start()
    wdn_own = wdp.at[pl.ds(0, 512), :]
    pltpu.make_async_copy(wdn_own, wdn_own, psem.at[3]).wait()
    remote(wdn_own, wdn_own, psem.at[4], psem.at[5], (d, mate)).wait_recv()
    k.wait()
    scatter(jnp.concatenate([hp[0], hp[1]], axis=1), wdp, zs2, zr2, z2sem)
    ov_h[...] = midway + arrived(zr2, z2sem)
    outs.append(pltpu.make_async_copy(ov_h, out_h, osem.at[4]))
    outs[4].start()

    part = idv.at[pl.ds(0, ND - 1)]
    remote(part, part, zsem.at[0], zsem.at[1], (d, mate)).wait_send()
    part = rows_s.at[pl.ds(0, ND - 1)]
    remote(part, part, zsem.at[2], zsem.at[3], (d, mate)).wait_send()
    for buf, sem, k in ((abuf, asem, a_fwd), (ebuf, esem, e_fwd), (fbuf, fsem, f_fwd), (mbuf, msem, m_fwd)):
        gather_sent(buf, sem)
        k.wait_send()

    @pl.loop(0, LOW)
    def _(j):
        @pl.when(j != me)
        def _():
            piece = wts.at[pl.ds(0, 32), :]
            remote(piece, piece, wsem.at[j], wrecv, (d, mate)).wait_send()

    @pl.when(me < LOW)
    def _():
        part = lt.at[pl.ds(0, NM - 1)]
        remote(part, part, ltsend, ltrecv.at[0], (d, mate)).wait_send()

    remote(wo_own, wo_own, psem.at[1], psem.at[2], (d, mate)).wait_send()
    remote(wdn_own, wdn_own, psem.at[4], psem.at[5], (d, mate)).wait_send()
    for buf, sem in ((zs, z1sem), (zs2, z2sem)):
        part = buf.at[pl.ds(0, NQ - 1)]
        remote(part, part, sem.at[0], sem.at[1], (d, mate)).wait_send()
    for k in outs:
        k.wait()


def per_device(
    ids, table, g1, b1, g2, b2, prior_rec, lerp, wd1, wd2, fbase, wa1, wa2, abase, wg1, wg2, erase, lcoef, reward,
    wr, wk, wv, state, clg, clb, wo, g3, b3, prior_ffn, lerp_ffn, wup, wdn,
):
    line = lambda x: x.reshape(1, 128)
    vocab = table.shape[0]
    operands = (
        ids.reshape(1, 64), table.reshape(vocab // 8, 8, 128), prior_rec, lerp, wd1, wd2, wa1, wa2, wg1, wg2,
        wr, wk, wv, state, wo, prior_ffn, wup, wdn,
        *map(line, (g1, b1, g2, b2, g3, b3, lerp_ffn, fbase, abase, erase, lcoef, reward, clg, clb)),
    )
    vmem = pltpu.VMEM
    dma = pltpu.SemaphoreType.DMA
    scratch = [
        vmem((ND, 1, 64), jnp.int32), pltpu.SMEM((ND, 1, 64), jnp.int32), vmem((vocab // 8, 8, 128), BF16),
        vmem((14, 1, 128), BF16), vmem((6, 128), BF16),
        vmem((128, 128), BF16), vmem((128, 128), BF16), vmem((128, 128), BF16), vmem((128, 128), BF16),
        vmem((128, 480), BF16), vmem((480, 128), BF16),
        vmem((N, 128), BF16), vmem((N, 128), BF16), vmem((N, 128), BF16), vmem((64, 2, 64, 64), F32),
        vmem((256, 2048), BF16), vmem((N, 512), BF16), vmem((1024, 2048), BF16),
        vmem((ND, 64, 128), BF16), vmem((ND, 64, 128), BF16),
        vmem((2, NQ, 80, 128), BF16), vmem((2, NQ, 64, 128), BF16), vmem((2, NQ, 64, 128), BF16), vmem((2, NQ, 64, 128), BF16),
        vmem((736, 128), BF16), vmem((32, N), BF16), vmem((4, 64, N), BF16), vmem((2, NQ, 64, 128), F32),
        vmem((NM, 32, 64), BF16), vmem((7, 2, 64, 128), F32), vmem((2, 64, 128), F32),
        vmem((2, 64, 128), BF16), vmem((64, 128), F32),
        vmem((NQ, 64, 128), BF16), vmem((NQ, 64, 128), BF16), vmem((NQ, 64, 128), BF16), vmem((NQ, 64, 128), BF16),
        vmem((2, 64, 512), BF16),
        vmem((64, 128), F32), vmem((64, 128), BF16), vmem((64, 128), BF16), vmem((64, 128), BF16),
        dma((32,)), dma((4,)), dma((4,)), dma((4,)), dma((4,)), dma((4,)), dma((LOW,)), dma, dma, dma((LOW,)),
        dma((6,)), dma((2,)), dma((2,)), dma((4,)), dma((5,)),
    ]
    anywhere = pl.BlockSpec(memory_space=pl.ANY)
    return pl.pallas_call(
        whole_step,
        name="whole_step",
        out_shape=(
            jax.ShapeDtypeStruct((64, 128), F32),
            jax.ShapeDtypeStruct(state.shape, F32),
            jax.ShapeDtypeStruct((64, 128), BF16),
            jax.ShapeDtypeStruct((64, 128), BF16),
            jax.ShapeDtypeStruct((64, 128), BF16),
        ),
        in_specs=[anywhere] * len(operands),
        out_specs=[anywhere] * 5,
        scratch_shapes=scratch,
        compiler_params=pltpu.CompilerParams(
            collective_id=0, has_side_effects=True, vmem_limit_bytes=60 << 20
        ),
    )(*operands)


def solution(mesh):
    col = P(None, "mp")
    row = P("mp", None)
    one = P("mp")
    both = P("dp", "mp")
    return jax.shard_map(
        per_device,
        mesh=mesh,
        in_specs=(
            P("dp"), both, one, one, one, one, both, col, row, col, one, row, col, one, row, col, one, one, one,
            col, col, col, P("dp", "mp", None, None), one, one, row, one, one, both, one, col, row,
        ),
        out_specs=(both, P("dp", "mp", None, None), both, both, both),
        check_vma=False,
    )
```

time: 215 us -> 80.5 us (0.37)
  Pallas kernels: 0 us -> 70 us
  other arithmetic: 45.8 us -> 0 us
  waiting for transfers between devices: 42.1 us -> 0 us
  blocking collectives: 38.7 us -> 0 us
  starting transfers between devices: 30.9 us -> 0 us
  matrix products: 15.6 us -> 0 us
  between operations: 15.9 us -> 0.64 us
  local copies, waits for them, and re-layouts: 24.6 us -> 9.68 us
    pallas_call x0 -> x1, Pallas kernels: none -> 70 us  [per_device(): pl.pallas_call(whole_step, name='whole_step', out_shape=(jax.ShapeDtypeSt...]
    all_to_all x4 -> x0, blocking collectives: 38.7 us -> none  [the longest x2 16.8 us: summed_on_arrival_2(): tiles = lax.all_to_all(in_blocks(x, dim, peers), axis, 0, 0, tiled=True)]
    all_to_all x6 -> x0, waiting for transfers between devices: 35.8 us -> none  [the longest x4 17.5 us: from_everyone(): lax.all_to_all(jnp.broadcast_to(x[None], (peers, *x.shape)), axis, 0, 0,...]
    all_to_all x6 -> x0, starting transfers between devices: 30.9 us -> none  [the longest x4 23.6 us: from_everyone(): lax.all_to_all(jnp.broadcast_to(x[None], (peers, *x.shape)), axis, 0, 0,...]
    mul x6 -> x0, other arithmetic: 22.2 us -> none  [the longest x1 19.8 us: recurrent_kernel(): removed[:, :, :, None] * (removal_key * alpha_heads)[:, :, None, :]]
    dot_general x10 -> x0, matrix products: 15.6 us -> none  [matmul(): return jnp.dot(left, right, preferred_element_type=jnp.float32)]
    convert_element_type x15 -> x0, other arithmetic: 14.5 us -> none  [the longest x2 1.65 us: per_device(): (att_base + shift_delta * recurrent_lerp_coefs[column].astype(jnp.float32...]
    unnamed x37 -> x12, local copies, waits for them, and re-layouts: 0.1 us -> 9.68 us
  transfers between devices with their start and end apart: 7 -> 0, of which waited for: 6 -> 0; matrix products, arithmetic and copies ran while one was open for 12% -> 0% of each run, Pallas kernels for 0% -> 0%
where the time goes in v1:
time: 80.5 us; the launch traced here: 80.3 us
  Pallas kernels  70 us (87%)
  local copies, waits for them, and re-layouts  9.68 us (12%)
    pallas_call x1, Pallas kernels, per_device(): pl.pallas_call(whole_step, name='whole_step', out_shape=(jax.ShapeDtypeSt...  70 us
    unnamed x12, local copies, waits for them, and re-layouts  9.68 us

profile of v1, /device:TPU:1, one launch (start us, length us, event | category | flops | bytes accessed | tf_op | source)
XLA Modules:
  0.0 80.3 jit_solution(10533704813094074289)
XLA Ops:
  0.6 1.7 %copy.37.wg1 = bf16[128,480]{1,0:T(8,128)(2,1)} copy(bf16[128,480]{0,1:T(8,128)(2,1)} %param.46) | data formatting | bytes 245760 | tf_op args[14]
  2.3 70.0 %whole_step.1 = (f32[64,128]{1,0:T(8,128)}, f32[64,2,64,64]{3,2,1,0:T(8,128)}, bf16[64,128]{1,0:T(8,128)(2,1)}, bf16[64,128]{1,0:T(8,128)(2,1)}, bf16[64,128]{1,0:T(8,128)(2,1)}) custom-call(s32[1,64]{1,0:T(1,128)} %bitcast.17, bf16[2048,8,128]{2,1,0:T(8,128)(2,1)} %bitcast.16, bf16[64,128]{1,0:T(8,128)(2,1)} %prior_rec.1, bf16[6,128]{1,0:T(8,128)(2,1)} %lerp.1, ...), custom_call_target="tpu_custom_call" | custom-call | tf_op jit(solution)/shard_map/whole_step/pallas_call | solution.py:494
  72.3 1.4 %copy.43 = f32[64,128]{1,0:T(8,128)} copy(f32[64,128]{1,0:T(8,128)} %get-tuple-element.10) | data formatting | bytes 65536
  73.7 0.0 copy-start.2
  73.7 0.0 copy-start.1
  73.7 0.0 copy-start
  73.7 4.8 %copy.44 = f32[64,2,64,64]{3,2,1,0:T(8,128)} copy(f32[64,2,64,64]{3,2,1,0:T(8,128)} %get-tuple-element.11) | data formatting | bytes 4194304
  78.5 0.0 copy-done.2
  78.5 0.6 copy.45
  79.1 0.0 copy-done.1
  79.1 0.6 copy.46
  79.7 0.0 copy-done
  79.7 0.6 copy.47
Async XLA Ops:
  73.7 4.8 %copy-start.2 = (bf16[64,128]{1,0:T(8,128)(2,1)S(1)}, bf16[64,128]{1,0:T(8,128)(2,1)}, u32[]{:S(2)}) copy-start(bf16[64,128]{1,0:T(8,128)(2,1)} %get-tuple-element.12) | copy-start | bytes 49156
  73.7 5.4 %copy-start.1 = (bf16[64,128]{1,0:T(8,128)(2,1)S(1)}, bf16[64,128]{1,0:T(8,128)(2,1)}, u32[]{:S(2)}) copy-start(bf16[64,128]{1,0:T(8,128)(2,1)} %get-tuple-element.13) | copy-start | bytes 49156
  73.7 6.0 %copy-start = (bf16[64,128]{1,0:T(8,128)(2,1)S(1)}, bf16[64,128]{1,0:T(8,128)(2,1)}, u32[]{:S(2)}) copy-start(bf16[64,128]{1,0:T(8,128)(2,1)} %get-tuple-element.14) | copy-start | bytes 49156

commit v2 on v1

--- a/solution.py
+++ b/solution.py
@@ -14,17 +14,17 @@
 ND = 4
 LOW = 23
 V_RK, V_DR, V_D, V_RKA, V_W, V_V, V_REM = range(7)
+VMEM_GRANT = 62_767_104
 E_HALF = 0.6065306597126334
 
 
 def whole_step(
     ids, table, prior_rec, lerp, wd1, wd2, wa1, wa2, wg1, wg2, wr, wk, wv, state, wo, prior_ffn, wup, wdn,
     g1, b1, g2, b2, g3, b3, lerp_ffn, fbase, abase, erase, lcoef, reward, clg, clb,
-    out_h, out_s, out_att, out_ffn, out_v,
-    idv, ids_s, tab, prm, lerp_v, wd1_v, wd2_v, wa1_v, wa2_v, wg1_v, wg2_v, wr_v, wk_v, wv_v, s_v,
+    ov_h, out_s, ov_att, ov_ffn, ov_v,
+    idv, ids_s, tab, prm, lerp_v, wd1_v, wd2_v, wa1_v, wa2_v, wg2_v, wr_v, wk_v, wv_v, s_v,
     wop, wup_v, wdp, rows_s, rows_r, abuf, ebuf, fbuf, mbuf, wts, wt, mx, res, lt, vec, rowb, ap, zf, zs, zr, zs2, zr2, hp,
-    ov_h, ov_att, ov_ffn, ov_v,
-    ld, zsem, asem, esem, fsem, msem, wsem, wrecv, ltsend, ltrecv, psem, z1sem, z2sem, hsem, osem,
+    ld, zsem, asem, esem, fsem, msem, wsem, wrecv, ltsend, ltrecv, psem, z1sem, z2sem, hsem,
 ):
     d = lax.axis_index("dp")
     me = lax.axis_index("mp")
@@ -55,7 +55,7 @@
     ]
     l_prm.append(load(lerp, lerp_v))
     l_prior = load(prior_rec, abuf.at[c, q, pl.ds(16, 64), :])
-    l_low = [load(wd1, wd1_v), load(wa1, wa1_v), load(wg1, wg1_v)]
+    l_low = [load(wd1, wd1_v), load(wa1, wa1_v), load(wg1, wts.at[pl.ds(256, 480), :])]
     l_tab = load(table, tab)
     l_rkv = [load(wk, wk_v), load(wv, wv_v), load(wr, wr_v)]
     l_s = load(state, s_v)
@@ -84,11 +84,6 @@
         k.wait()
     wts[0:128, :] = jnp.transpose(wd1_v[...].astype(F32)).astype(BF16)
     wts[128:256, :] = jnp.transpose(wa1_v[...].astype(F32)).astype(BF16)
-    for t in range(3):
-        wts[256 + 128 * t : 384 + 128 * t, :] = jnp.transpose(
-            wg1_v[:, 128 * t : 128 * t + 128].astype(F32)
-        ).astype(BF16)
-    wts[640:736, :] = jnp.transpose(wg1_v[:, 384:480].astype(F32)).astype(BF16)
     l_ids.wait()
     l_prior.wait()
 
@@ -175,9 +170,11 @@
     base = d * tab.shape[0] * 8
     sub8 = lax.broadcasted_iota(jnp.int32, (8, 128), 0)
 
-    for s in range(ND):
-        @pl.loop(0, 8)
-        def _(g, s=s):
+    for i in range(ND):
+        s = (d + 1 + i) % ND
+
+        @pl.loop(0, 8, unroll=4)
+        def _(g, s=s, i=i):
             block = jnp.zeros((8, 128), F32)
             for u in range(8):
                 at = ids_s[s, 0, g * 8 + u] - base
@@ -187,18 +184,13 @@
                 want = jnp.where(inside, at % 8, 8)
                 row = jnp.sum(jnp.where(sub8 == want, eight, 0.0), axis=0, keepdims=True)
                 block = jnp.where(sub8 == u, row, block)
-            rowb[0, pl.ds(pl.multiple_of(g * 8, 8), 8), :] = block
-
-        rows_s[s] = rowb[0].astype(BF16)
-
-        @pl.when(d != s)
-        def _(s=s):
+            rowb[i % 2, pl.ds(pl.multiple_of(g * 8, 8), 8), :] = block
+
+        if i < ND - 1:
+            rows_s[s] = rowb[i % 2].astype(BF16)
             remote(rows_s.at[s], rows_r.at[d], zsem.at[2], zsem.at[3], (s, me)).start()
-
-    for s in range(ND):
-        @pl.when(d == s)
-        def _(s=s):
-            rows_r[s] = rows_s[s]
+        else:
+            rows_r[d] = rowb[i % 2].astype(BF16)
 
     a_fwd = gather_finish(abuf, asem)
 
@@ -260,8 +252,6 @@
     over_blocks(mixing, 0)
     own_res = res[c, q]
     ov_att[...] = ((own_res - mean2) * inv2 * par(2) + par(3)).astype(BF16)
-    outs = [pltpu.make_async_copy(ov_att, out_att, osem.at[0])]
-    outs[0].start()
 
     @pl.when(me < LOW)
     def _():
@@ -290,7 +280,7 @@
         return jnp.dot(mx[i], w[...], preferred_element_type=F32)
 
     def state_times(i):
-        @pl.loop(0, 64)
+        @pl.loop(0, 64, unroll=8)
         def _(b):
             for h in (0, 1):
                 col = rowsum(s_v[b, h] * vec[i, h, pl.ds(b, 1), 0:64])
@@ -304,8 +294,6 @@
     values = projected(2, wv_v, l_rkv[1])
     recept = projected(3, wr_v, l_rkv[2])
     ov_v[...] = values.astype(BF16)
-    outs.append(pltpu.make_async_copy(ov_v, out_v, osem.at[1]))
-    outs[1].start()
     head_rows(V_RK, removal)
     head_rows(V_V, values)
     rowb[0] = zero
@@ -382,16 +370,14 @@
 
     scatter(jnp.concatenate([ap[0], ap[1]], axis=1), wop, zs, zr, z1sem)
 
-    @pl.loop(0, 64)
+    @pl.loop(0, 64, unroll=4)
     def _(b):
         for h in (0, 1):
             row = lambda i: vec[i, h, pl.ds(b, 1), 0:64]
             gone = rowsum(jnp.where(eye, row(V_REM), 0.0))
             val = rowsum(jnp.where(eye, row(V_V), 0.0))
-            s_v[b, h] = s_v[b, h] * row(V_D) - gone * row(V_RKA) + val * row(V_W)
-
-    outs.append(pltpu.make_async_copy(s_v, out_s, osem.at[2]))
-    outs[2].start()
+            out_s[b, h] = s_v[b, h] * row(V_D) - gone * row(V_RKA) + val * row(V_W)
+
 
     f_fwd = gather_finish(fbuf, fsem)
     midway = own_res + arrived(zr, z1sem)
@@ -419,16 +405,12 @@
     k = remote(hp.at[c], hp.at[c], hsem.at[2], hsem.at[3], (d, mate))
     k.start()
     ov_ffn[...] = ((midway - mean3) * inv3 * par(4) + par(5)).astype(BF16)
-    outs.append(pltpu.make_async_copy(ov_ffn, out_ffn, osem.at[3]))
-    outs[3].start()
     wdn_own = wdp.at[pl.ds(0, 512), :]
     pltpu.make_async_copy(wdn_own, wdn_own, psem.at[3]).wait()
     remote(wdn_own, wdn_own, psem.at[4], psem.at[5], (d, mate)).wait_recv()
     k.wait()
     scatter(jnp.concatenate([hp[0], hp[1]], axis=1), wdp, zs2, zr2, z2sem)
     ov_h[...] = midway + arrived(zr2, z2sem)
-    outs.append(pltpu.make_async_copy(ov_h, out_h, osem.at[4]))
-    outs[4].start()
 
     part = idv.at[pl.ds(0, ND - 1)]
     remote(part, part, zsem.at[0], zsem.at[1], (d, mate)).wait_send()
@@ -455,7 +437,14 @@
     for buf, sem in ((zs, z1sem), (zs2, z2sem)):
         part = buf.at[pl.ds(0, NQ - 1)]
         remote(part, part, sem.at[0], sem.at[1], (d, mate)).wait_send()
-    for k in outs:
+
+
+def write_out(*refs):
+    sem = refs[10]
+    copies = [pltpu.make_async_copy(refs[i], refs[5 + i], sem.at[i]) for i in range(5)]
+    for k in copies:
+        k.start()
+    for k in copies:
         k.wait()
 
 
@@ -466,7 +455,7 @@
     line = lambda x: x.reshape(1, 128)
     vocab = table.shape[0]
     operands = (
-        ids.reshape(1, 64), table.reshape(vocab // 8, 8, 128), prior_rec, lerp, wd1, wd2, wa1, wa2, wg1, wg2,
+        ids.reshape(1, 64), table.reshape(vocab // 8, 8, 128), prior_rec, lerp, wd1, wd2, wa1, wa2, wg1.T, wg2,
         wr, wk, wv, state, wo, prior_ffn, wup, wdn,
         *map(line, (g1, b1, g2, b2, g3, b3, lerp_ffn, fbase, abase, erase, lcoef, reward, clg, clb)),
     )
@@ -476,7 +465,7 @@
         vmem((ND, 1, 64), jnp.int32), pltpu.SMEM((ND, 1, 64), jnp.int32), vmem((vocab // 8, 8, 128), BF16),
         vmem((14, 1, 128), BF16), vmem((6, 128), BF16),
         vmem((128, 128), BF16), vmem((128, 128), BF16), vmem((128, 128), BF16), vmem((128, 128), BF16),
-        vmem((128, 480), BF16), vmem((480, 128), BF16),
+        vmem((480, 128), BF16),
         vmem((N, 128), BF16), vmem((N, 128), BF16), vmem((N, 128), BF16), vmem((64, 2, 64, 64), F32),
         vmem((256, 2048), BF16), vmem((N, 512), BF16), vmem((1024, 2048), BF16),
         vmem((ND, 64, 128), BF16), vmem((ND, 64, 128), BF16),
@@ -486,28 +475,32 @@
         vmem((2, 64, 128), BF16), vmem((64, 128), F32),
         vmem((NQ, 64, 128), BF16), vmem((NQ, 64, 128), BF16), vmem((NQ, 64, 128), BF16), vmem((NQ, 64, 128), BF16),
         vmem((2, 64, 512), BF16),
-        vmem((64, 128), F32), vmem((64, 128), BF16), vmem((64, 128), BF16), vmem((64, 128), BF16),
         dma((32,)), dma((4,)), dma((4,)), dma((4,)), dma((4,)), dma((4,)), dma((LOW,)), dma, dma, dma((LOW,)),
-        dma((6,)), dma((2,)), dma((2,)), dma((4,)), dma((5,)),
+        dma((6,)), dma((2,)), dma((2,)), dma((4,)),
     ]
-    anywhere = pl.BlockSpec(memory_space=pl.ANY)
-    return pl.pallas_call(
+    anywhere = pl.BlockSpec(memory_space=pltpu.HBM)
+    inside = pl.BlockSpec(memory_space=pltpu.VMEM)
+    shapes = (((64, 128), F32), (state.shape, F32), ((64, 128), BF16), ((64, 128), BF16), ((64, 128), BF16))
+    kept = pl.pallas_call(
         whole_step,
         name="whole_step",
-        out_shape=(
-            jax.ShapeDtypeStruct((64, 128), F32),
-            jax.ShapeDtypeStruct(state.shape, F32),
-            jax.ShapeDtypeStruct((64, 128), BF16),
-            jax.ShapeDtypeStruct((64, 128), BF16),
-            jax.ShapeDtypeStruct((64, 128), BF16),
-        ),
+        out_shape=tuple(pltpu.VMEM(*x) for x in shapes),
         in_specs=[anywhere] * len(operands),
-        out_specs=[anywhere] * 5,
+        out_specs=[inside] * 5,
         scratch_shapes=scratch,
         compiler_params=pltpu.CompilerParams(
-            collective_id=0, has_side_effects=True, vmem_limit_bytes=60 << 20
+            collective_id=0, has_side_effects=True, vmem_limit_bytes=VMEM_GRANT
         ),
     )(*operands)
+    return pl.pallas_call(
+        write_out,
+        name="write_out",
+        out_shape=tuple(jax.ShapeDtypeStruct(*x) for x in shapes),
+        in_specs=[inside] * 5,
+        out_specs=[anywhere] * 5,
+        scratch_shapes=[dma((5,))],
+        compiler_params=pltpu.CompilerParams(vmem_limit_bytes=1 << 20),
+    )(*kept)
 
 
 def solution(mesh):

time: 80.5 us -> 63.2 us (0.79)
  local copies, waits for them, and re-layouts: 9.68 us -> 0 us
  Pallas kernels: 70 us -> 62.5 us
    unnamed x12 -> x0, local copies, waits for them, and re-layouts: 9.68 us -> none
    pallas_call x1 -> x2, Pallas kernels: 70 us -> 62.5 us  [the longest x1 60.4 us: per_device(): pl.pallas_call(whole_step, name='whole_step', out_shape=tuple((pltpu.VMEM...]
where the time goes in v2:
time: 63.2 us; the launch traced here: 63.1 us
  Pallas kernels  62.5 us (99%)
  between operations  0.65 us (1%)
    pallas_call x1, Pallas kernels, per_device(): pl.pallas_call(whole_step, name='whole_step', out_shape=tuple((pltpu.VMEM...  60.4 us
    pallas_call x1, Pallas kernels, per_device(): pl.pallas_call(write_out, name='write_out', out_shape=tuple((jax.ShapeDty...  2.08 us

profile of v2, /device:TPU:1, one launch (start us, length us, event | category | flops | bytes accessed | tf_op | source)
XLA Modules:
  0.0 63.1 jit_solution(11753051076405277050)
XLA Ops:
  0.6 60.4 %whole_step.1 = (f32[64,128]{1,0:T(8,128)S(1)}, f32[64,2,64,64]{3,2,1,0:T(8,128)S(1)}, bf16[64,128]{1,0:T(8,128)(2,1)S(1)}, bf16[64,128]{1,0:T(8,128)(2,1)S(1)}, bf16[64,128]{1,0:T(8,128)(2,1)S(1)}) custom-call(s32[1,64]{1,0:T(1,128)} %bitcast.19, bf16[2048,8,128]{2,1,0:T(8,128)(2,1)} %bitcast.17, bf16[64,128]{1,0:T(8,128)(2,1)} %prior_rec.1, ...), custom_call_target="tpu_custom_call" | custom-call | tf_op jit(solution)/shard_map/whole_step/pallas_call | solution.py:484
  61.1 2.1 %write_out.1 = (f32[64,128]{1,0:T(8,128)}, f32[64,2,64,64]{3,2,1,0:T(8,128)}, bf16[64,128]{1,0:T(8,128)(2,1)}, bf16[64,128]{1,0:T(8,128)(2,1)}, bf16[64,128]{1,0:T(8,128)(2,1)}) custom-call(f32[64,128]{1,0:T(8,128)S(1)} %get-tuple-element.10.refs_0_, f32[64,2,64,64]{3,2,1,0:T(8,128)S(1)} %get-tuple-element.11.refs_1_, ...), custom_call_target="tpu_custom_call" | custom-call | tf_op jit(solution)/shard_map/write_out/pallas_call | solution.py:495

commit v3 on v2

--- a/solution.py
+++ b/solution.py
@@ -15,6 +15,10 @@
 LOW = 23
 V_RK, V_DR, V_D, V_RKA, V_W, V_V, V_REM = range(7)
 VMEM_GRANT = 62_767_104
+FAR = sorted(
+    ((dy, dx) for dy in range(4) for dx in range(4) if dy or dx),
+    key=lambda o: -min(o[0], 4 - o[0]) - min(o[1], 4 - o[1]),
+)
 E_HALF = 0.6065306597126334
 
 
@@ -23,8 +27,8 @@
     g1, b1, g2, b2, g3, b3, lerp_ffn, fbase, abase, erase, lcoef, reward, clg, clb,
     ov_h, out_s, ov_att, ov_ffn, ov_v,
     idv, ids_s, tab, prm, lerp_v, wd1_v, wd2_v, wa1_v, wa2_v, wg2_v, wr_v, wk_v, wv_v, s_v,
-    wop, wup_v, wdp, rows_s, rows_r, abuf, ebuf, fbuf, mbuf, wts, wt, mx, res, lt, vec, rowb, ap, zf, zs, zr, zs2, zr2, hp,
-    ld, zsem, asem, esem, fsem, msem, wsem, wrecv, ltsend, ltrecv, psem, z1sem, z2sem, hsem,
+    wop, wup_v, wdp, rows_s, rows_r, abuf, ebuf, fbuf, mbuf, wts, wt, mx, res, att, lt, vec, rowb, ap, zf, zs, zr, zs2, zr2, hp,
+    ld, zsem, asem, esem, fsem, msem, agot, egot, fgot, mgot, wsem, wrecv, ltsend, ltrecv, psem, z1sem, z2sem, hsem,
 ):
     d = lax.axis_index("dp")
     me = lax.axis_index("mp")
@@ -39,6 +43,17 @@
 
     def lanes(i):
         return pl.ds(pl.multiple_of(i * 128, 128), 128)
+
+    def chip(dy, dx):
+        return (q // 4 + dy) % 4 * 4 + (q % 4 + dx) % 4
+
+    barrier = pltpu.get_barrier_semaphore()
+    for i in range(1, ND):
+        pl.semaphore_signal(barrier, inc=1, device_id=((d + i) % ND, me), device_id_type=MESH)
+    for dy, dx in FAR:
+        for e in (0, 1):
+            pl.semaphore_signal(barrier, inc=1, device_id=(d, 2 * chip(dy, dx) + e), device_id_type=MESH)
+    pl.semaphore_signal(barrier, inc=1, device_id=(d, mate), device_id_type=MESH)
 
     loads = []
 
@@ -61,16 +76,6 @@
     l_s = load(state, s_v)
     l_low2 = [load(wd2, wd2_v), load(wa2, wa2_v), load(wg2, wg2_v)]
     l_priorf = load(prior_ffn, fbuf.at[c, q])
-
-    barrier = pltpu.get_barrier_semaphore()
-
-    @pl.loop(1, ND)
-    def _(i):
-        pl.semaphore_signal(barrier, inc=1, device_id=((d + i) % ND, me), device_id_type=MESH)
-
-    @pl.loop(1, NM)
-    def _(i):
-        pl.semaphore_signal(barrier, inc=1, device_id=(d, (me + i) % NM), device_id_type=MESH)
 
     for k in l_prm:
         k.wait()
@@ -93,23 +98,28 @@
     def _(i):
         remote(idv.at[d], idv.at[d], zsem.at[0], zsem.at[1], ((d + i) % ND, me)).start()
 
-    def gather_start(buf, sem):
-        @pl.loop(1, NQ)
-        def _(i):
-            remote(buf.at[c, q], buf.at[c, q], sem.at[0], sem.at[1], (d, 2 * ((q + i) % NQ) + c)).start()
-
-    def gather_finish(buf, sem):
+    def gather_start(buf, sem, got):
+        for dy, dx in FAR:
+            remote(buf.at[c, q], buf.at[c, q], sem.at[0], got.at[q], (d, 2 * chip(dy, dx) + 1 - c)).start()
+        remote(buf.at[c, q], buf.at[c, q], sem.at[0], got.at[q], (d, mate)).start()
+
+    def gather_pass_on(buf, sem, got):
+        for dy, dx in FAR[::-1]:
+            t = chip(dy, dx)
+            remote(buf.at[1 - c, t], buf.at[1 - c, t], sem.at[0], got.at[t], (d, mate)).wait_recv()
+            remote(buf.at[1 - c, t], buf.at[1 - c, t], sem.at[1], sem.at[2], (d, mate)).start()
+
+    def gather_end(buf, sem, got):
+        remote(buf.at[1 - c, q], buf.at[1 - c, q], sem.at[0], got.at[q], (d, mate)).wait_recv()
         part = buf.at[0, pl.ds(0, NQ - 1)]
-        remote(part, part, sem.at[0], sem.at[1], (d, mate)).wait_recv()
-        k = remote(buf.at[c], buf.at[c], sem.at[2], sem.at[3], (d, mate))
-        k.start()
-        return k
+        remote(part, part, sem.at[1], sem.at[2], (d, mate)).wait_recv()
 
     def gather_sent(buf, sem):
+        remote(buf.at[0], buf.at[0], sem.at[0], sem.at[2], (d, mate)).wait_send()
         part = buf.at[0, pl.ds(0, NQ - 1)]
-        remote(part, part, sem.at[0], sem.at[1], (d, mate)).wait_send()
-
-    gather_start(abuf, asem)
+        remote(part, part, sem.at[1], sem.at[2], (d, mate)).wait_send()
+
+    gather_start(abuf, asem, agot)
 
     @pl.loop(0, LOW)
     def _(j):
@@ -128,24 +138,24 @@
         own_w.append(
             (
                 pltpu.make_async_copy(
-                    wo.at[:, lanes(2 * t + c)],
+                    wo.at[:, lanes(2 * t + 1 - c)],
                     wop.at[pl.ds(pl.multiple_of(c * 128, 128), 128), pl.ds(t * 128, 128)],
                     psem.at[0],
                 ),
                 remote(
-                    wo.at[:, lanes(2 * t + 1 - c)],
+                    wo.at[:, lanes(2 * t + c)],
                     wop.at[pl.ds(pl.multiple_of(c * 128, 128), 128), pl.ds(t * 128, 128)],
                     psem.at[1],
                     psem.at[2],
                     (d, mate),
                 ),
                 pltpu.make_async_copy(
-                    wdn.at[:, lanes(2 * t + c)],
+                    wdn.at[:, lanes(2 * t + 1 - c)],
                     wdp.at[pl.ds(pl.multiple_of(c * 512, 512), 512), pl.ds(t * 128, 128)],
                     psem.at[3],
                 ),
                 remote(
-                    wdn.at[:, lanes(2 * t + 1 - c)],
+                    wdn.at[:, lanes(2 * t + c)],
                     wdp.at[pl.ds(pl.multiple_of(c * 512, 512), 512), pl.ds(t * 128, 128)],
                     psem.at[4],
                     psem.at[5],
@@ -167,7 +177,7 @@
     k.start()
     l_tab.wait()
     k.wait()
-    base = d * tab.shape[0] * 8
+    bits = (tab.shape[0] * 8).bit_length() - 1
     sub8 = lax.broadcasted_iota(jnp.int32, (8, 128), 0)
 
     for i in range(ND):
@@ -177,11 +187,9 @@
         def _(g, s=s, i=i):
             block = jnp.zeros((8, 128), F32)
             for u in range(8):
-                at = ids_s[s, 0, g * 8 + u] - base
-                inside = jnp.logical_and(at >= 0, at < tab.shape[0] * 8)
-                at = jnp.where(inside, at, 0)
-                eight = tab[at // 8].astype(F32)
-                want = jnp.where(inside, at % 8, 8)
+                token = ids_s[s, 0, g * 8 + u]
+                eight = tab[lax.shift_right_logical(token, 3) & (tab.shape[0] - 1)].astype(F32)
+                want = jnp.where(lax.shift_right_logical(token, bits) == d, token & 7, 8)
                 row = jnp.sum(jnp.where(sub8 == want, eight, 0.0), axis=0, keepdims=True)
                 block = jnp.where(sub8 == u, row, block)
             rowb[i % 2, pl.ds(pl.multiple_of(g * 8, 8), 8), :] = block
@@ -192,7 +200,7 @@
         else:
             rows_r[d] = rowb[i % 2].astype(BF16)
 
-    a_fwd = gather_finish(abuf, asem)
+    gather_pass_on(abuf, asem, agot)
 
     part = rows_r.at[pl.ds(0, ND - 1)]
     remote(part, part, zsem.at[2], zsem.at[3], (d, mate)).wait_recv()
@@ -200,12 +208,11 @@
     for s in range(1, ND):
         found = found + rows_r[s].astype(F32)
     ebuf[c, q] = found.astype(BF16)
-    gather_start(ebuf, esem)
+    gather_start(ebuf, esem, egot)
+    gather_end(abuf, asem, agot)
     l_priorf.wait()
-    gather_start(fbuf, fsem)
-    e_fwd = gather_finish(ebuf, esem)
-    a_fwd.wait_recv()
-    e_fwd.wait_recv()
+    gather_pass_on(ebuf, esem, egot)
+    gather_end(ebuf, esem, egot)
 
     def params(cc, t):
         return abuf[cc, t, 0:16, :].astype(F32)
@@ -239,19 +246,15 @@
 
     def mixing(cc, t, acc):
         p = params(cc, t)
-        att = ((res[cc, t] - mean2) * inv2 * p[2:3] + p[3:4]).astype(BF16).astype(F32)
-        delta = abuf[cc, t, 16:80, :].astype(F32) - att
+        base = ((res[cc, t] - mean2) * inv2 * p[2:3] + p[3:4]).astype(BF16)
+        att[cc, t] = base
+        base = base.astype(F32)
         low = jnp.where(me < 4, p[5:6], jnp.where(me < 8, p[8:9], p[9:10]))
-        at = lanes(2 * t + cc)
-        mx[0, :, at] = (att + delta * low).astype(BF16)
-        mx[1, :, at] = (att + delta * p[6:7]).astype(BF16)
-        mx[2, :, at] = (att + delta * p[7:8]).astype(BF16)
-        mx[3, :, at] = (att + delta * p[4:5]).astype(BF16)
+        mx[0, :, lanes(2 * t + cc)] = (base + (abuf[cc, t, 16:80, :].astype(F32) - base) * low).astype(BF16)
         return acc
 
     over_blocks(mixing, 0)
     own_res = res[c, q]
-    ov_att[...] = ((own_res - mean2) * inv2 * par(2) + par(3)).astype(BF16)
 
     @pl.when(me < LOW)
     def _():
@@ -259,11 +262,26 @@
         remote(got, got, wsem.at[0], wrecv, (d, mate)).wait_recv()
         low = lax.dot_general(wt[...], mx[0], (((1,), (1,)), ((), ())), preferred_element_type=F32)
         low = jnp.where(me < 4, jnp.tanh(low), jnp.where(me < 8, low, jax.nn.sigmoid(low)))
-        lt[me] = low.astype(BF16)
-
-        @pl.loop(1, NM)
-        def _(i):
-            remote(lt.at[me], lt.at[me], ltsend, ltrecv.at[me], (d, (me + i) % NM)).start()
+        lt[me] = jnp.concatenate([low[0:16], low[16:32]], axis=1).astype(BF16)
+        for dy, dx in FAR:
+            for e in (0, 1):
+                remote(lt.at[me], lt.at[me], ltsend, ltrecv.at[me], (d, 2 * chip(dy, dx) + e)).start()
+        remote(lt.at[me], lt.at[me], ltsend, ltrecv.at[me], (d, mate)).start()
+
+    gather_start(fbuf, fsem, fgot)
+
+    def mixing_rest(cc, t, acc):
+        p = params(cc, t)
+        base = att[cc, t].astype(F32)
+        delta = abuf[cc, t, 16:80, :].astype(F32) - base
+        at = lanes(2 * t + cc)
+        mx[1, :, at] = (base + delta * p[6:7]).astype(BF16)
+        mx[2, :, at] = (base + delta * p[7:8]).astype(BF16)
+        mx[3, :, at] = (base + delta * p[4:5]).astype(BF16)
+        return acc
+
+    over_blocks(mixing_rest, 0)
+    ov_att[...] = att[c, q]
 
     def head_rows(i, x):
         vec[i, 0] = x
@@ -312,8 +330,12 @@
             remote(lt.at[j], lt.at[j], ltsend, ltrecv.at[j], (d, mate)).wait_recv()
 
     def second(lo, hi, w):
-        low = lt[lo:hi].astype(F32).reshape((hi - lo) * 32, 64)
-        return jnp.dot(jnp.transpose(low).astype(BF16), w[...], preferred_element_type=F32)
+        n = hi - lo
+        low = jnp.transpose(lt[lo:hi].astype(F32).reshape(n * 16, 128)).astype(BF16)
+        parts = [jnp.concatenate([w[32 * j + 16 * u : 32 * j + 16 * u + 16, :] for j in range(n)], axis=0) for u in (0, 1)]
+        return jnp.dot(low[0:64], parts[0], preferred_element_type=F32) + jnp.dot(
+            low[64:128], parts[1], preferred_element_type=F32
+        )
 
     decay = jnp.exp(-E_HALF * jax.nn.sigmoid(par(7) + second(0, 4, wd2_v)))
     alpha = jax.nn.sigmoid(par(8) + second(4, 8, wa2_v))
@@ -337,38 +359,31 @@
     wo_own = wop.at[pl.ds(0, 128), :]
     pltpu.make_async_copy(wo_own, wo_own, psem.at[0]).wait()
     remote(wo_own, wo_own, psem.at[1], psem.at[2], (d, mate)).wait_recv()
-    k.wait()
-
-    def scatter(pair, w, send, recv, sem):
-        @pl.loop(0, NQ // 2)
-        def _(i):
-            t = (i + q // 2) % (NQ // 2)
-            y = jnp.dot(
-                pair, w[:, pl.ds(pl.multiple_of(t * 256, 256), 256)], preferred_element_type=F32
-            )
+    def scatter(own, pair, w, width, send, recv, sem, k):
+        rows_own = pl.ds(pl.multiple_of(c * width, width), width)
+        rows_mate = pl.ds(pl.multiple_of((1 - c) * width, width), width)
+        chunks = [(dy, dx) for dy in (2, 1, 3, 0) for dx in (1, 0)]
+        place = [(q // 4 + dy) % 4 * 2 + (q % 4 // 2 + dx) % 2 for dy, dx in chunks]
+        cols = [pl.ds(pl.multiple_of(t * 256, 256), 256) for t in place]
+        for i in range(8):
+            zf[i] = jnp.dot(own, w[rows_own, cols[i]], preferred_element_type=F32)
+        k.wait()
+        other = pair[1 - c]
+        for i in range(8):
+            y = zf[i] + jnp.dot(other, w[rows_mate, cols[i]], preferred_element_type=F32)
             for u in (0, 1):
-                to = 2 * t + u
-                block = y[:, 128 * u : 128 * u + 128]
-                send[to] = block.astype(BF16)
-
-                @pl.when(to != q)
-                def _(to=to):
-                    remote(send.at[to], recv.at[q], sem.at[0], sem.at[1], (d, 2 * to + c)).start()
-
-                @pl.when(to == q)
-                def _(block=block):
-                    zf[...] = block
-                    recv[q] = jnp.zeros((64, 128), BF16)
+                to = 2 * place[i] + u
+                send[to] = y[:, 128 * u : 128 * u + 128].astype(BF16)
+                remote(send.at[to], recv.at[q], sem.at[0], sem.at[1], (d, 2 * to + 1 - c)).start()
 
     def arrived(recv, sem):
-        part = recv.at[pl.ds(0, NQ - 1)]
-        remote(part, part, sem.at[0], sem.at[1], (d, mate)).wait_recv()
-        total = zf[...]
-        for t in range(NQ):
+        remote(recv, recv, sem.at[0], sem.at[1], (d, mate)).wait_recv()
+        total = recv[0].astype(F32)
+        for t in range(1, NQ):
             total = total + recv[t].astype(F32)
         return total
 
-    scatter(jnp.concatenate([ap[0], ap[1]], axis=1), wop, zs, zr, z1sem)
+    scatter(ap[c], ap, wop, 128, zs, zr, z1sem, k)
 
     @pl.loop(0, 64, unroll=4)
     def _(b):
@@ -379,13 +394,13 @@
             out_s[b, h] = s_v[b, h] * row(V_D) - gone * row(V_RKA) + val * row(V_W)
 
 
-    f_fwd = gather_finish(fbuf, fsem)
+    gather_pass_on(fbuf, fsem, fgot)
     midway = own_res + arrived(zr, z1sem)
     mbuf[c, q] = midway.astype(BF16)
-    gather_start(mbuf, msem)
-    f_fwd.wait_recv()
-    m_fwd = gather_finish(mbuf, msem)
-    m_fwd.wait_recv()
+    gather_start(mbuf, msem, mgot)
+    gather_end(fbuf, fsem, fgot)
+    gather_pass_on(mbuf, msem, mgot)
+    gather_end(mbuf, msem, mgot)
 
     mean3 = rowsum(over_blocks(lambda cc, t, acc: acc + mbuf[cc, t].astype(F32), zero)) / N
     inv3 = lax.rsqrt(
@@ -408,17 +423,15 @@
     wdn_own = wdp.at[pl.ds(0, 512), :]
     pltpu.make_async_copy(wdn_own, wdn_own, psem.at[3]).wait()
     remote(wdn_own, wdn_own, psem.at[4], psem.at[5], (d, mate)).wait_recv()
-    k.wait()
-    scatter(jnp.concatenate([hp[0], hp[1]], axis=1), wdp, zs2, zr2, z2sem)
+    scatter(hp[c], hp, wdp, 512, zs2, zr2, z2sem, k)
     ov_h[...] = midway + arrived(zr2, z2sem)
 
     part = idv.at[pl.ds(0, ND - 1)]
     remote(part, part, zsem.at[0], zsem.at[1], (d, mate)).wait_send()
     part = rows_s.at[pl.ds(0, ND - 1)]
     remote(part, part, zsem.at[2], zsem.at[3], (d, mate)).wait_send()
-    for buf, sem, k in ((abuf, asem, a_fwd), (ebuf, esem, e_fwd), (fbuf, fsem, f_fwd), (mbuf, msem, m_fwd)):
+    for buf, sem in ((abuf, asem), (ebuf, esem), (fbuf, fsem), (mbuf, msem)):
         gather_sent(buf, sem)
-        k.wait_send()
 
     @pl.loop(0, LOW)
     def _(j):
@@ -435,8 +448,7 @@
     remote(wo_own, wo_own, psem.at[1], psem.at[2], (d, mate)).wait_send()
     remote(wdn_own, wdn_own, psem.at[4], psem.at[5], (d, mate)).wait_send()
     for buf, sem in ((zs, z1sem), (zs2, z2sem)):
-        part = buf.at[pl.ds(0, NQ - 1)]
-        remote(part, part, sem.at[0], sem.at[1], (d, mate)).wait_send()
+        remote(buf, buf, sem.at[0], sem.at[1], (d, mate)).wait_send()
 
 
 def write_out(*refs):
@@ -471,11 +483,11 @@
         vmem((ND, 64, 128), BF16), vmem((ND, 64, 128), BF16),
         vmem((2, NQ, 80, 128), BF16), vmem((2, NQ, 64, 128), BF16), vmem((2, NQ, 64, 128), BF16), vmem((2, NQ, 64, 128), BF16),
         vmem((736, 128), BF16), vmem((32, N), BF16), vmem((4, 64, N), BF16), vmem((2, NQ, 64, 128), F32),
-        vmem((NM, 32, 64), BF16), vmem((7, 2, 64, 128), F32), vmem((2, 64, 128), F32),
-        vmem((2, 64, 128), BF16), vmem((64, 128), F32),
+        vmem((2, NQ, 64, 128), BF16), vmem((NM, 16, 128), BF16), vmem((7, 2, 64, 128), F32), vmem((2, 64, 128), F32),
+        vmem((2, 64, 128), BF16), vmem((8, 64, 256), F32),
         vmem((NQ, 64, 128), BF16), vmem((NQ, 64, 128), BF16), vmem((NQ, 64, 128), BF16), vmem((NQ, 64, 128), BF16),
         vmem((2, 64, 512), BF16),
-        dma((32,)), dma((4,)), dma((4,)), dma((4,)), dma((4,)), dma((4,)), dma((LOW,)), dma, dma, dma((LOW,)),
+        dma((32,)), dma((4,)), dma((3,)), dma((3,)), dma((3,)), dma((3,)), dma((NQ,)), dma((NQ,)), dma((NQ,)), dma((NQ,)), dma((LOW,)), dma, dma, dma((LOW,)),
         dma((6,)), dma((2,)), dma((2,)), dma((4,)),
     ]
     anywhere = pl.BlockSpec(memory_space=pltpu.HBM)

time: 63.2 us -> 58.7 us (0.929)
  Pallas kernels: 62.5 us -> 58 us
    pallas_call x1, Pallas kernels: 60.4 us -> 55.9 us  [per_device(): pl.pallas_call(whole_step, name='whole_step', out_shape=tuple((pltpu.VMEM...]
where the time goes in v3:
time: 58.7 us; the launch traced here: 58.6 us
  Pallas kernels  58 us (99%)
  between operations  0.65 us (1%)
    pallas_call x1, Pallas kernels, per_device(): pl.pallas_call(whole_step, name='whole_step', out_shape=tuple((pltpu.VMEM...  55.9 us
    pallas_call x1, Pallas kernels, per_device(): pl.pallas_call(write_out, name='write_out', out_shape=tuple((jax.ShapeDty...  2.08 us

profile of v3, /device:TPU:1, one launch (start us, length us, event | category | flops | bytes accessed | tf_op | source)
XLA Modules:
  0.0 58.6 jit_solution(2547530038274979795)
XLA Ops:
  0.6 55.9 %whole_step.1 = (f32[64,128]{1,0:T(8,128)S(1)}, f32[64,2,64,64]{3,2,1,0:T(8,128)S(1)}, bf16[64,128]{1,0:T(8,128)(2,1)S(1)}, bf16[64,128]{1,0:T(8,128)(2,1)S(1)}, bf16[64,128]{1,0:T(8,128)(2,1)S(1)}) custom-call(s32[1,64]{1,0:T(1,128)} %bitcast.19, bf16[2048,8,128]{2,1,0:T(8,128)(2,1)} %bitcast.17, bf16[64,128]{1,0:T(8,128)(2,1)} %prior_rec.1, ...), custom_call_target="tpu_custom_call" | custom-call | tf_op jit(solution)/shard_map/whole_step/pallas_call | solution.py:496
  56.5 2.1 %write_out.1 = (f32[64,128]{1,0:T(8,128)}, f32[64,2,64,64]{3,2,1,0:T(8,128)}, bf16[64,128]{1,0:T(8,128)(2,1)}, bf16[64,128]{1,0:T(8,128)(2,1)}, bf16[64,128]{1,0:T(8,128)(2,1)}) custom-call(f32[64,128]{1,0:T(8,128)S(1)} %get-tuple-element.10.refs_0_, f32[64,2,64,64]{3,2,1,0:T(8,128)S(1)} %get-tuple-element.11.refs_1_, ...), custom_call_target="tpu_custom_call" | custom-call | tf_op jit(solution)/shard_map/write_out/pallas_call | solution.py:507

commit v4 on v3

--- a/solution.py
+++ b/solution.py
@@ -13,7 +13,7 @@
 NM = 32
 ND = 4
 LOW = 23
-V_RK, V_DR, V_D, V_RKA, V_W, V_V, V_REM = range(7)
+V_D, V_RKA, V_W, V_V, V_REM = range(5)
 VMEM_GRANT = 62_767_104
 FAR = sorted(
     ((dy, dx) for dy in range(4) for dx in range(4) if dy or dx),
@@ -27,7 +27,7 @@
     g1, b1, g2, b2, g3, b3, lerp_ffn, fbase, abase, erase, lcoef, reward, clg, clb,
     ov_h, out_s, ov_att, ov_ffn, ov_v,
     idv, ids_s, tab, prm, lerp_v, wd1_v, wd2_v, wa1_v, wa2_v, wg2_v, wr_v, wk_v, wv_v, s_v,
-    wop, wup_v, wdp, rows_s, rows_r, abuf, ebuf, fbuf, mbuf, wts, wt, mx, res, att, lt, vec, rowb, ap, zf, zs, zr, zs2, zr2, hp,
+    wop, wup_v, wdp, si, st, rows_s, rows_r, abuf, ebuf, fbuf, mbuf, wts, wt, mx, res, att, lt, vec, rowb, ap, zf, zs, zr, zs2, zr2, hp,
     ld, zsem, asem, esem, fsem, msem, agot, egot, fgot, mgot, wsem, wrecv, ltsend, ltrecv, psem, z1sem, z2sem, hsem,
 ):
     d = lax.axis_index("dp")
@@ -49,7 +49,8 @@
 
     barrier = pltpu.get_barrier_semaphore()
     for i in range(1, ND):
-        pl.semaphore_signal(barrier, inc=1, device_id=((d + i) % ND, me), device_id_type=MESH)
+        for m in (me, mate):
+            pl.semaphore_signal(barrier, inc=1, device_id=((d + i) % ND, m), device_id_type=MESH)
     for dy, dx in FAR:
         for e in (0, 1):
             pl.semaphore_signal(barrier, inc=1, device_id=(d, 2 * chip(dy, dx) + e), device_id_type=MESH)
@@ -72,8 +73,6 @@
     l_prior = load(prior_rec, abuf.at[c, q, pl.ds(16, 64), :])
     l_low = [load(wd1, wd1_v), load(wa1, wa1_v), load(wg1, wts.at[pl.ds(256, 480), :])]
     l_tab = load(table, tab)
-    l_rkv = [load(wk, wk_v), load(wv, wv_v), load(wr, wr_v)]
-    l_s = load(state, s_v)
     l_low2 = [load(wd2, wd2_v), load(wa2, wa2_v), load(wg2, wg2_v)]
     l_priorf = load(prior_ffn, fbuf.at[c, q])
 
@@ -89,25 +88,33 @@
         k.wait()
     wts[0:128, :] = jnp.transpose(wd1_v[...].astype(F32)).astype(BF16)
     wts[128:256, :] = jnp.transpose(wa1_v[...].astype(F32)).astype(BF16)
+    @pl.loop(0, 64)
+    def _(i):
+        for h in (0, 1):
+            pltpu.make_async_copy(state.at[:, h, i, :], si.at[i, h], psem.at[6]).start()
+
+    l_rkv = [load(wk, wk_v), load(wv, wv_v), load(wr, wr_v)]
     l_ids.wait()
     l_prior.wait()
 
-    pl.semaphore_wait(barrier, ND - 1 + NM - 1)
-
-    @pl.loop(1, ND)
-    def _(i):
-        remote(idv.at[d], idv.at[d], zsem.at[0], zsem.at[1], ((d + i) % ND, me)).start()
+    pl.semaphore_wait(barrier, 2 * (ND - 1) + NM - 1)
+
+    for i in (2, 1, 3):
+        remote(idv.at[d], idv.at[d], zsem.at[0], zsem.at[1], ((d + i) % ND, mate)).start()
 
     def gather_start(buf, sem, got):
         for dy, dx in FAR:
             remote(buf.at[c, q], buf.at[c, q], sem.at[0], got.at[q], (d, 2 * chip(dy, dx) + 1 - c)).start()
         remote(buf.at[c, q], buf.at[c, q], sem.at[0], got.at[q], (d, mate)).start()
 
-    def gather_pass_on(buf, sem, got):
+    def gather_pass_on(buf, sem, got, use=None, acc=None):
         for dy, dx in FAR[::-1]:
             t = chip(dy, dx)
             remote(buf.at[1 - c, t], buf.at[1 - c, t], sem.at[0], got.at[t], (d, mate)).wait_recv()
             remote(buf.at[1 - c, t], buf.at[1 - c, t], sem.at[1], sem.at[2], (d, mate)).start()
+            if use is not None:
+                acc = use(1 - c, t, acc)
+        return acc
 
     def gather_end(buf, sem, got):
         remote(buf.at[1 - c, q], buf.at[1 - c, q], sem.at[0], got.at[q], (d, mate)).wait_recv()
@@ -166,6 +173,7 @@
     for k in own_w:
         k[0].start()
         k[1].start()
+    l_s = load(state, s_v)
     l_up = load(wup, wup_v)
     for k in own_w:
         k[2].start()
@@ -181,7 +189,7 @@
     sub8 = lax.broadcasted_iota(jnp.int32, (8, 128), 0)
 
     for i in range(ND):
-        s = (d + 1 + i) % ND
+        s = (d + (2, 1, 3, 0)[i]) % ND
 
         @pl.loop(0, 8, unroll=4)
         def _(g, s=s, i=i):
@@ -200,7 +208,6 @@
         else:
             rows_r[d] = rowb[i % 2].astype(BF16)
 
-    gather_pass_on(abuf, asem, agot)
 
     part = rows_r.at[pl.ds(0, ND - 1)]
     remote(part, part, zsem.at[2], zsem.at[3], (d, mate)).wait_recv()
@@ -209,15 +216,39 @@
         found = found + rows_r[s].astype(F32)
     ebuf[c, q] = found.astype(BF16)
     gather_start(ebuf, esem, egot)
+    gather_pass_on(abuf, asem, agot)
     gather_end(abuf, asem, agot)
     l_priorf.wait()
-    gather_pass_on(ebuf, esem, egot)
-    gather_end(ebuf, esem, egot)
+    def rowsum(x):
+        return jnp.sum(x, axis=-1, keepdims=True)
+
+    zero = jnp.zeros((64, 128), F32)
+
+    def moments_of(buf):
+        pivot = rowsum(buf[c, q].astype(F32)) / 128
+
+        def add(cc, t, acc):
+            x = buf[cc, t].astype(F32) - pivot
+            return acc[0] + x, acc[1] + x * x
+
+        return pivot, add
+
+    def mean_and_scale(pivot, acc):
+        shift = rowsum(acc[0]) / N
+        return pivot + shift, lax.rsqrt(jnp.maximum(rowsum(acc[1]) / N - shift * shift, 0.0) + 1e-05)
+
+    def gathered_norm(buf, sem, got):
+        pivot, add = moments_of(buf)
+        acc = gather_pass_on(buf, sem, got, add, (zero, zero))
+        gather_end(buf, sem, got)
+        acc = add(1 - c, q, acc)
+        acc = lax.fori_loop(0, NQ, lambda t, acc: add(c, t, acc), acc, unroll=4)
+        return mean_and_scale(pivot, acc)
+
+    mean1, inv1 = gathered_norm(ebuf, esem, egot)
 
     def params(cc, t):
         return abuf[cc, t, 0:16, :].astype(F32)
-
-    zero = jnp.zeros((64, 128), F32)
 
     def over_blocks(body, init):
         def step(t, acc):
@@ -227,41 +258,42 @@
 
         return lax.fori_loop(0, NQ, step, init)
 
-    def rowsum(x):
-        return jnp.sum(x, axis=-1, keepdims=True)
-
-    mean1 = rowsum(over_blocks(lambda cc, t, acc: acc + ebuf[cc, t].astype(F32), zero)) / N
-    inv1 = lax.rsqrt(
-        rowsum(over_blocks(lambda cc, t, acc: acc + jnp.square(ebuf[cc, t].astype(F32) - mean1), zero)) / N + 1e-05
-    )
+    own_p = params(c, q)
+    own_res = (ebuf[c, q].astype(F32) - mean1) * inv1 * own_p[0:1] + own_p[1:2]
+    pivot2 = rowsum(own_res) / 128
 
     def first_norm(cc, t, acc):
         p = params(cc, t)
         r = (ebuf[cc, t].astype(F32) - mean1) * inv1 * p[0:1] + p[1:2]
         res[cc, t] = r
-        return acc + r
-
-    mean2 = rowsum(over_blocks(first_norm, zero)) / N
-    inv2 = lax.rsqrt(rowsum(over_blocks(lambda cc, t, acc: acc + jnp.square(res[cc, t] - mean2), zero)) / N + 1e-05)
-
-    def mixing(cc, t, acc):
+        r = r - pivot2
+        return acc[0] + r, acc[1] + r * r
+
+    mean2, inv2 = mean_and_scale(pivot2, over_blocks(first_norm, (zero, zero)))
+
+    @pl.when(me < LOW)
+    def _():
+        got = wt.at[:, pl.ds(0, (NM - 1) * 128)]
+        remote(got, got, wsem.at[0], wrecv, (d, mate)).wait_recv()
+
+    def mixing(cc, t):
         p = params(cc, t)
         base = ((res[cc, t] - mean2) * inv2 * p[2:3] + p[3:4]).astype(BF16)
         att[cc, t] = base
         base = base.astype(F32)
-        low = jnp.where(me < 4, p[5:6], jnp.where(me < 8, p[8:9], p[9:10]))
-        mx[0, :, lanes(2 * t + cc)] = (base + (abuf[cc, t, 16:80, :].astype(F32) - base) * low).astype(BF16)
-        return acc
-
-    over_blocks(mixing, 0)
-    own_res = res[c, q]
+        rate = jnp.where(me < 4, p[5:6], jnp.where(me < 8, p[8:9], p[9:10]))
+        return (base + (abuf[cc, t, 16:80, :].astype(F32) - base) * rate).astype(BF16)
+
+    low = 0.0
+    for t in range(NQ):
+        x = jnp.concatenate([mixing(0, t), mixing(1, t)], axis=1)
+        low = low + lax.dot_general(
+            wt[:, 256 * t : 256 * t + 256], x, (((1,), (1,)), ((), ())), preferred_element_type=F32
+        )
+    low = jnp.where(me < 4, jnp.tanh(low), jnp.where(me < 8, low, jax.nn.sigmoid(low)))
 
     @pl.when(me < LOW)
     def _():
-        got = wt.at[:, pl.ds(0, (NM - 1) * 128)]
-        remote(got, got, wsem.at[0], wrecv, (d, mate)).wait_recv()
-        low = lax.dot_general(wt[...], mx[0], (((1,), (1,)), ((), ())), preferred_element_type=F32)
-        low = jnp.where(me < 4, jnp.tanh(low), jnp.where(me < 8, low, jax.nn.sigmoid(low)))
         lt[me] = jnp.concatenate([low[0:16], low[16:32]], axis=1).astype(BF16)
         for dy, dx in FAR:
             for e in (0, 1):
@@ -297,14 +329,18 @@
         k.wait()
         return jnp.dot(mx[i], w[...], preferred_element_type=F32)
 
-    def state_times(i):
+    def turned(x):
+        y = jnp.transpose(x)
+        return jnp.concatenate([y[0:64], y[64:128]], axis=1)
+
+    def state_times(x):
+        y = turned(x)
+
         @pl.loop(0, 64, unroll=8)
-        def _(b):
-            for h in (0, 1):
-                col = rowsum(s_v[b, h] * vec[i, h, pl.ds(b, 1), 0:64])
-                rowb[h, pl.ds(b, 1), 0:64] = jnp.sum(jnp.where(eye, col, 0.0), axis=0, keepdims=True)
-
-        return jnp.where(left, rowb[0], pltpu.roll(rowb[1], 64, axis=1))
+        def _(i):
+            rowb[0, pl.ds(i, 1), :] = jnp.sum(st[i] * y, axis=0, keepdims=True)
+
+        return turned(rowb[0])
 
     keys = projected(1, wk_v, l_rkv[0])
     removal = keys * par(9)
@@ -312,12 +348,14 @@
     values = projected(2, wv_v, l_rkv[1])
     recept = projected(3, wr_v, l_rkv[2])
     ov_v[...] = values.astype(BF16)
-    head_rows(V_RK, removal)
     head_rows(V_V, values)
-    rowb[0] = zero
-    rowb[1] = zero
-    l_s.wait()
-    removed = state_times(V_RK)
+    pltpu.make_async_copy(si, si, psem.at[6]).wait()
+
+    @pl.loop(0, 64, unroll=4)
+    def _(i):
+        st[i] = jnp.transpose(si[i].reshape(128, 64))
+
+    removed = state_times(removal)
     head_rows(V_REM, removed)
 
     for k in l_low2:
@@ -345,9 +383,8 @@
     head_rows(V_D, decay)
     head_rows(V_RKA, rka)
     head_rows(V_W, written)
-    head_rows(V_DR, decay * recept)
     readout = (
-        state_times(V_DR) - removed * headsum(rka * recept) + values * headsum(written * recept)
+        state_times(decay * recept) - removed * headsum(rka * recept) + values * headsum(written * recept)
     )
     centered = readout - headsum(readout) / 64
     normed = centered * lax.rsqrt(headsum(centered * centered) / 64 + 0.00064) * par(12) + par(13)
@@ -362,18 +399,19 @@
     def scatter(own, pair, w, width, send, recv, sem, k):
         rows_own = pl.ds(pl.multiple_of(c * width, width), width)
         rows_mate = pl.ds(pl.multiple_of((1 - c) * width, width), width)
-        chunks = [(dy, dx) for dy in (2, 1, 3, 0) for dx in (1, 0)]
-        place = [(q // 4 + dy) % 4 * 2 + (q % 4 // 2 + dx) % 2 for dy, dx in chunks]
-        cols = [pl.ds(pl.multiple_of(t * 256, 256), 256) for t in place]
-        for i in range(8):
+        rows = [(q // 4 + dy) % 4 for dy in (2, 1, 3, 0)]
+        cols = [pl.ds(pl.multiple_of(t * 512, 512), 512) for t in rows]
+        for i in range(4):
             zf[i] = jnp.dot(own, w[rows_own, cols[i]], preferred_element_type=F32)
         k.wait()
         other = pair[1 - c]
-        for i in range(8):
+        for i in range(4):
             y = zf[i] + jnp.dot(other, w[rows_mate, cols[i]], preferred_element_type=F32)
-            for u in (0, 1):
-                to = 2 * place[i] + u
+            for u in range(4):
+                to = 4 * rows[i] + u
                 send[to] = y[:, 128 * u : 128 * u + 128].astype(BF16)
+            for u in range(4):
+                to = 4 * rows[i] + u
                 remote(send.at[to], recv.at[q], sem.at[0], sem.at[1], (d, 2 * to + 1 - c)).start()
 
     def arrived(recv, sem):
@@ -384,6 +422,8 @@
         return total
 
     scatter(ap[c], ap, wop, 128, zs, zr, z1sem, k)
+
+    l_s.wait()
 
     @pl.loop(0, 64, unroll=4)
     def _(b):
@@ -399,23 +439,18 @@
     mbuf[c, q] = midway.astype(BF16)
     gather_start(mbuf, msem, mgot)
     gather_end(fbuf, fsem, fgot)
-    gather_pass_on(mbuf, msem, mgot)
-    gather_end(mbuf, msem, mgot)
-
-    mean3 = rowsum(over_blocks(lambda cc, t, acc: acc + mbuf[cc, t].astype(F32), zero)) / N
-    inv3 = lax.rsqrt(
-        rowsum(over_blocks(lambda cc, t, acc: acc + jnp.square(mbuf[cc, t].astype(F32) - mean3), zero)) / N + 1e-05
-    )
-
-    def ffn_mixing(cc, t, acc):
+    mean3, inv3 = gathered_norm(mbuf, msem, mgot)
+
+    def ffn_mixed(cc, t):
         p = params(cc, t)
         base = ((mbuf[cc, t].astype(F32) - mean3) * inv3 * p[10:11] + p[11:12]).astype(BF16).astype(F32)
-        mx[0, :, lanes(2 * t + cc)] = (base + (fbuf[cc, t].astype(F32) - base) * p[12:13]).astype(BF16)
-        return acc
-
-    over_blocks(ffn_mixing, 0)
+        return (base + (fbuf[cc, t].astype(F32) - base) * p[12:13]).astype(BF16)
+
     l_up.wait()
-    up = jnp.dot(mx[0], wup_v[...], preferred_element_type=F32)
+    up = 0.0
+    for t in range(NQ):
+        x = jnp.concatenate([ffn_mixed(0, t), ffn_mixed(1, t)], axis=1)
+        up = up + jnp.dot(x, wup_v[256 * t : 256 * t + 256, :], preferred_element_type=F32)
     hp[c] = jnp.square(jnp.maximum(up, 0.0)).astype(BF16)
     k = remote(hp.at[c], hp.at[c], hsem.at[2], hsem.at[3], (d, mate))
     k.start()
@@ -453,7 +488,10 @@
 
 def write_out(*refs):
     sem = refs[10]
-    copies = [pltpu.make_async_copy(refs[i], refs[5 + i], sem.at[i]) for i in range(5)]
+    copies = [pltpu.make_async_copy(refs[i], refs[5 + i], sem.at[i]) for i in (0, 2, 3, 4)]
+    for i in range(8):
+        part = pl.ds(8 * i, 8)
+        copies.append(pltpu.make_async_copy(refs[1].at[part], refs[6].at[part], sem.at[5 + i]))
     for k in copies:
         k.start()
     for k in copies:
@@ -480,15 +518,16 @@
         vmem((480, 128), BF16),
         vmem((N, 128), BF16), vmem((N, 128), BF16), vmem((N, 128), BF16), vmem((64, 2, 64, 64), F32),
         vmem((256, 2048), BF16), vmem((N, 512), BF16), vmem((1024, 2048), BF16),
+        vmem((64, 2, 64, 64), F32), vmem((64, 64, 128), F32),
         vmem((ND, 64, 128), BF16), vmem((ND, 64, 128), BF16),
         vmem((2, NQ, 80, 128), BF16), vmem((2, NQ, 64, 128), BF16), vmem((2, NQ, 64, 128), BF16), vmem((2, NQ, 64, 128), BF16),
         vmem((736, 128), BF16), vmem((32, N), BF16), vmem((4, 64, N), BF16), vmem((2, NQ, 64, 128), F32),
-        vmem((2, NQ, 64, 128), BF16), vmem((NM, 16, 128), BF16), vmem((7, 2, 64, 128), F32), vmem((2, 64, 128), F32),
-        vmem((2, 64, 128), BF16), vmem((8, 64, 256), F32),
+        vmem((2, NQ, 64, 128), BF16), vmem((NM, 16, 128), BF16), vmem((5, 2, 64, 128), F32), vmem((2, 64, 128), F32),
+        vmem((2, 64, 128), BF16), vmem((4, 64, 512), F32),
         vmem((NQ, 64, 128), BF16), vmem((NQ, 64, 128), BF16), vmem((NQ, 64, 128), BF16), vmem((NQ, 64, 128), BF16),
         vmem((2, 64, 512), BF16),
         dma((32,)), dma((4,)), dma((3,)), dma((3,)), dma((3,)), dma((3,)), dma((NQ,)), dma((NQ,)), dma((NQ,)), dma((NQ,)), dma((LOW,)), dma, dma, dma((LOW,)),
-        dma((6,)), dma((2,)), dma((2,)), dma((4,)),
+        dma((7,)), dma((2,)), dma((2,)), dma((4,)),
     ]
     anywhere = pl.BlockSpec(memory_space=pltpu.HBM)
     inside = pl.BlockSpec(memory_space=pltpu.VMEM)
@@ -510,7 +549,7 @@
         out_shape=tuple(jax.ShapeDtypeStruct(*x) for x in shapes),
         in_specs=[inside] * 5,
         out_specs=[anywhere] * 5,
-        scratch_shapes=[dma((5,))],
+        scratch_shapes=[dma((13,))],
         compiler_params=pltpu.CompilerParams(vmem_limit_bytes=1 << 20),
     )(*kept)
 

time: 58.7 us -> 56.5 us (0.963)
  Pallas kernels: 58 us -> 55.7 us
    pallas_call x1, Pallas kernels: 55.9 us -> 53.6 us  [per_device(): pl.pallas_call(whole_step, name='whole_step', out_shape=tuple((pltpu.VMEM...]
where the time goes in v4:
time: 56.5 us; the launch traced here: 56.4 us
  Pallas kernels  55.7 us (99%)
  between operations  0.65 us (1%)
    pallas_call x1, Pallas kernels, per_device(): pl.pallas_call(whole_step, name='whole_step', out_shape=tuple((pltpu.VMEM...  53.6 us
    pallas_call x1, Pallas kernels, per_device(): pl.pallas_call(write_out, name='write_out', out_shape=tuple((jax.ShapeDty...  2.14 us

profile of v4, /device:TPU:1, one launch (start us, length us, event | category | flops | bytes accessed | tf_op | source)
XLA Modules:
  0.0 56.4 jit_solution(7378500678704689792)
XLA Ops:
  0.6 53.6 %whole_step.1 = (f32[64,128]{1,0:T(8,128)S(1)}, f32[64,2,64,64]{3,2,1,0:T(8,128)S(1)}, bf16[64,128]{1,0:T(8,128)(2,1)S(1)}, bf16[64,128]{1,0:T(8,128)(2,1)S(1)}, bf16[64,128]{1,0:T(8,128)(2,1)S(1)}) custom-call(s32[1,64]{1,0:T(1,128)} %bitcast.19, bf16[2048,8,128]{2,1,0:T(8,128)(2,1)} %bitcast.17, bf16[64,128]{1,0:T(8,128)(2,1)} %prior_rec.1, ...), custom_call_target="tpu_custom_call" | custom-call | tf_op jit(solution)/shard_map/whole_step/pallas_call | solution.py:535
  54.2 2.1 %write_out.1 = (f32[64,128]{1,0:T(8,128)}, f32[64,2,64,64]{3,2,1,0:T(8,128)}, bf16[64,128]{1,0:T(8,128)(2,1)}, bf16[64,128]{1,0:T(8,128)(2,1)}, bf16[64,128]{1,0:T(8,128)(2,1)}) custom-call(f32[64,128]{1,0:T(8,128)S(1)} %get-tuple-element.10.refs_0_, f32[64,2,64,64]{3,2,1,0:T(8,128)S(1)} %get-tuple-element.11.refs_1_, ...), custom_call_target="tpu_custom_call" | custom-call | tf_op jit(solution)/shard_map/write_out/pallas_call | solution.py:546

commit v5 on v4

--- a/solution.py
+++ b/solution.py
@@ -102,22 +102,22 @@
     for i in (2, 1, 3):
         remote(idv.at[d], idv.at[d], zsem.at[0], zsem.at[1], ((d + i) % ND, mate)).start()
 
-    def gather_start(buf, sem, got):
+    def gather_start(buf, sem, got, p):
         for dy, dx in FAR:
-            remote(buf.at[c, q], buf.at[c, q], sem.at[0], got.at[q], (d, 2 * chip(dy, dx) + 1 - c)).start()
-        remote(buf.at[c, q], buf.at[c, q], sem.at[0], got.at[q], (d, mate)).start()
-
-    def gather_pass_on(buf, sem, got, use=None, acc=None):
+            remote(buf.at[p, q], buf.at[p, q], sem.at[0], got.at[q], (d, 2 * chip(dy, dx) + 1 - c)).start()
+        remote(buf.at[p, q], buf.at[p, q], sem.at[0], got.at[q], (d, mate)).start()
+
+    def gather_pass_on(buf, sem, got, p, use=None, acc=None):
         for dy, dx in FAR[::-1]:
             t = chip(dy, dx)
-            remote(buf.at[1 - c, t], buf.at[1 - c, t], sem.at[0], got.at[t], (d, mate)).wait_recv()
-            remote(buf.at[1 - c, t], buf.at[1 - c, t], sem.at[1], sem.at[2], (d, mate)).start()
+            remote(buf.at[1 - p, t], buf.at[1 - p, t], sem.at[0], got.at[t], (d, mate)).wait_recv()
+            remote(buf.at[1 - p, t], buf.at[1 - p, t], sem.at[1], sem.at[2], (d, mate)).start()
             if use is not None:
-                acc = use(1 - c, t, acc)
+                acc = use(1 - p, t, acc)
         return acc
 
-    def gather_end(buf, sem, got):
-        remote(buf.at[1 - c, q], buf.at[1 - c, q], sem.at[0], got.at[q], (d, mate)).wait_recv()
+    def gather_end(buf, sem, got, p):
+        remote(buf.at[1 - p, q], buf.at[1 - p, q], sem.at[0], got.at[q], (d, mate)).wait_recv()
         part = buf.at[0, pl.ds(0, NQ - 1)]
         remote(part, part, sem.at[1], sem.at[2], (d, mate)).wait_recv()
 
@@ -126,7 +126,7 @@
         part = buf.at[0, pl.ds(0, NQ - 1)]
         remote(part, part, sem.at[1], sem.at[2], (d, mate)).wait_send()
 
-    gather_start(abuf, asem, agot)
+    gather_start(abuf, asem, agot, c)
 
     @pl.loop(0, LOW)
     def _(j):
@@ -202,30 +202,25 @@
                 block = jnp.where(sub8 == u, row, block)
             rowb[i % 2, pl.ds(pl.multiple_of(g * 8, 8), 8), :] = block
 
-        if i < ND - 1:
-            rows_s[s] = rowb[i % 2].astype(BF16)
-            remote(rows_s.at[s], rows_r.at[d], zsem.at[2], zsem.at[3], (s, me)).start()
-        else:
-            rows_r[d] = rowb[i % 2].astype(BF16)
-
-
-    part = rows_r.at[pl.ds(0, ND - 1)]
-    remote(part, part, zsem.at[2], zsem.at[3], (d, mate)).wait_recv()
+        rows_s[s] = rowb[i % 2].astype(BF16)
+        remote(rows_s.at[s], rows_r.at[d], zsem.at[2], zsem.at[3], (s, mate)).start()
+
+    remote(rows_r, rows_r, zsem.at[2], zsem.at[3], (d, mate)).wait_recv()
     found = rows_r[0].astype(F32)
     for s in range(1, ND):
         found = found + rows_r[s].astype(F32)
-    ebuf[c, q] = found.astype(BF16)
-    gather_start(ebuf, esem, egot)
-    gather_pass_on(abuf, asem, agot)
-    gather_end(abuf, asem, agot)
+    ebuf[1 - c, q] = found.astype(BF16)
+    gather_start(ebuf, esem, egot, 1 - c)
+    gather_pass_on(abuf, asem, agot, c)
+    gather_end(abuf, asem, agot, c)
     l_priorf.wait()
     def rowsum(x):
         return jnp.sum(x, axis=-1, keepdims=True)
 
     zero = jnp.zeros((64, 128), F32)
 
-    def moments_of(buf):
-        pivot = rowsum(buf[c, q].astype(F32)) / 128
+    def moments_of(buf, p):
+        pivot = rowsum(buf[p, q].astype(F32)) / 128
 
         def add(cc, t, acc):
             x = buf[cc, t].astype(F32) - pivot
@@ -237,15 +232,15 @@
         shift = rowsum(acc[0]) / N
         return pivot + shift, lax.rsqrt(jnp.maximum(rowsum(acc[1]) / N - shift * shift, 0.0) + 1e-05)
 
-    def gathered_norm(buf, sem, got):
-        pivot, add = moments_of(buf)
-        acc = gather_pass_on(buf, sem, got, add, (zero, zero))
-        gather_end(buf, sem, got)
-        acc = add(1 - c, q, acc)
-        acc = lax.fori_loop(0, NQ, lambda t, acc: add(c, t, acc), acc, unroll=4)
+    def gathered_norm(buf, sem, got, p):
+        pivot, add = moments_of(buf, p)
+        acc = gather_pass_on(buf, sem, got, p, add, (zero, zero))
+        gather_end(buf, sem, got, p)
+        acc = add(1 - p, q, acc)
+        acc = lax.fori_loop(0, NQ, lambda t, acc: add(p, t, acc), acc, unroll=4)
         return mean_and_scale(pivot, acc)
 
-    mean1, inv1 = gathered_norm(ebuf, esem, egot)
+    mean1, inv1 = gathered_norm(ebuf, esem, egot, 1 - c)
 
     def params(cc, t):
         return abuf[cc, t, 0:16, :].astype(F32)
@@ -300,7 +295,7 @@
                 remote(lt.at[me], lt.at[me], ltsend, ltrecv.at[me], (d, 2 * chip(dy, dx) + e)).start()
         remote(lt.at[me], lt.at[me], ltsend, ltrecv.at[me], (d, mate)).start()
 
-    gather_start(fbuf, fsem, fgot)
+    gather_start(fbuf, fsem, fgot, c)
 
     def mixing_rest(cc, t, acc):
         p = params(cc, t)
@@ -396,22 +391,30 @@
     wo_own = wop.at[pl.ds(0, 128), :]
     pltpu.make_async_copy(wo_own, wo_own, psem.at[0]).wait()
     remote(wo_own, wo_own, psem.at[1], psem.at[2], (d, mate)).wait_recv()
-    def scatter(own, pair, w, width, send, recv, sem, k):
-        rows_own = pl.ds(pl.multiple_of(c * width, width), width)
-        rows_mate = pl.ds(pl.multiple_of((1 - c) * width, width), width)
+    def scatter(own, other, w, width, send, recv, sem, copies):
+        step = width // len(own)
+
+        def rows_of(p, i):
+            return pl.ds(pl.multiple_of(p * width + i * step, step), step)
+
         rows = [(q // 4 + dy) % 4 for dy in (2, 1, 3, 0)]
         cols = [pl.ds(pl.multiple_of(t * 512, 512), 512) for t in rows]
+        terms = [(x, rows_of(c, i)) for i, x in enumerate(own)]
+        j = len(own) - 1
+        for i in range(j):
+            copies[i].wait()
+            terms.append((other(i), rows_of(1 - c, i)))
         for i in range(4):
-            zf[i] = jnp.dot(own, w[rows_own, cols[i]], preferred_element_type=F32)
-        k.wait()
-        other = pair[1 - c]
+            zf[i] = sum(jnp.dot(x, w[r, cols[i]], preferred_element_type=F32) for x, r in terms)
+        copies[j].wait()
+        last = other(j)
         for i in range(4):
-            y = zf[i] + jnp.dot(other, w[rows_mate, cols[i]], preferred_element_type=F32)
+            y = zf[i] + jnp.dot(last, w[rows_of(1 - c, j), cols[i]], preferred_element_type=F32)
             for u in range(4):
                 to = 4 * rows[i] + u
                 send[to] = y[:, 128 * u : 128 * u + 128].astype(BF16)
-            for u in range(4):
-                to = 4 * rows[i] + u
+            for dx in (2, 1, 3, 0):
+                to = 4 * rows[i] + (q % 4 + dx) % 4
                 remote(send.at[to], recv.at[q], sem.at[0], sem.at[1], (d, 2 * to + 1 - c)).start()
 
     def arrived(recv, sem):
@@ -421,7 +424,7 @@
             total = total + recv[t].astype(F32)
         return total
 
-    scatter(ap[c], ap, wop, 128, zs, zr, z1sem, k)
+    scatter([ap[c]], lambda i: ap[1 - c], wop, 128, zs, zr, z1sem, [k])
 
     l_s.wait()
 
@@ -434,12 +437,12 @@
             out_s[b, h] = s_v[b, h] * row(V_D) - gone * row(V_RKA) + val * row(V_W)
 
 
-    gather_pass_on(fbuf, fsem, fgot)
+    gather_pass_on(fbuf, fsem, fgot, c)
     midway = own_res + arrived(zr, z1sem)
     mbuf[c, q] = midway.astype(BF16)
-    gather_start(mbuf, msem, mgot)
-    gather_end(fbuf, fsem, fgot)
-    mean3, inv3 = gathered_norm(mbuf, msem, mgot)
+    gather_start(mbuf, msem, mgot, c)
+    gather_end(fbuf, fsem, fgot, c)
+    mean3, inv3 = gathered_norm(mbuf, msem, mgot, c)
 
     def ffn_mixed(cc, t):
         p = params(cc, t)
@@ -450,21 +453,24 @@
     up = 0.0
     for t in range(NQ):
         x = jnp.concatenate([ffn_mixed(0, t), ffn_mixed(1, t)], axis=1)
-        up = up + jnp.dot(x, wup_v[256 * t : 256 * t + 256, :], preferred_element_type=F32)
-    hp[c] = jnp.square(jnp.maximum(up, 0.0)).astype(BF16)
-    k = remote(hp.at[c], hp.at[c], hsem.at[2], hsem.at[3], (d, mate))
-    k.start()
+        mx[0, :, 256 * t : 256 * t + 256] = x
+        up = up + jnp.dot(x, wup_v[256 * t : 256 * t + 256, 0:256], preferred_element_type=F32)
+    hp[0, c] = jnp.square(jnp.maximum(up, 0.0)).astype(BF16)
+    halves = [remote(hp.at[i, c], hp.at[i, c], hsem.at[2 + 2 * i], hsem.at[3 + 2 * i], (d, mate)) for i in (0, 1)]
+    halves[0].start()
+    up = jnp.dot(mx[0], wup_v[:, 256:512], preferred_element_type=F32)
+    hp[1, c] = jnp.square(jnp.maximum(up, 0.0)).astype(BF16)
+    halves[1].start()
     ov_ffn[...] = ((midway - mean3) * inv3 * par(4) + par(5)).astype(BF16)
     wdn_own = wdp.at[pl.ds(0, 512), :]
     pltpu.make_async_copy(wdn_own, wdn_own, psem.at[3]).wait()
     remote(wdn_own, wdn_own, psem.at[4], psem.at[5], (d, mate)).wait_recv()
-    scatter(hp[c], hp, wdp, 512, zs2, zr2, z2sem, k)
+    scatter([hp[0, c], hp[1, c]], lambda i: hp[i, 1 - c], wdp, 512, zs2, zr2, z2sem, halves)
     ov_h[...] = midway + arrived(zr2, z2sem)
 
     part = idv.at[pl.ds(0, ND - 1)]
     remote(part, part, zsem.at[0], zsem.at[1], (d, mate)).wait_send()
-    part = rows_s.at[pl.ds(0, ND - 1)]
-    remote(part, part, zsem.at[2], zsem.at[3], (d, mate)).wait_send()
+    remote(rows_s, rows_s, zsem.at[2], zsem.at[3], (d, mate)).wait_send()
     for buf, sem in ((abuf, asem), (ebuf, esem), (fbuf, fsem), (mbuf, msem)):
         gather_sent(buf, sem)
 
@@ -525,9 +531,9 @@
         vmem((2, NQ, 64, 128), BF16), vmem((NM, 16, 128), BF16), vmem((5, 2, 64, 128), F32), vmem((2, 64, 128), F32),
         vmem((2, 64, 128), BF16), vmem((4, 64, 512), F32),
         vmem((NQ, 64, 128), BF16), vmem((NQ, 64, 128), BF16), vmem((NQ, 64, 128), BF16), vmem((NQ, 64, 128), BF16),
-        vmem((2, 64, 512), BF16),
+        vmem((2, 2, 64, 256), BF16),
         dma((32,)), dma((4,)), dma((3,)), dma((3,)), dma((3,)), dma((3,)), dma((NQ,)), dma((NQ,)), dma((NQ,)), dma((NQ,)), dma((LOW,)), dma, dma, dma((LOW,)),
-        dma((7,)), dma((2,)), dma((2,)), dma((4,)),
+        dma((7,)), dma((2,)), dma((2,)), dma((6,)),
     ]
     anywhere = pl.BlockSpec(memory_space=pltpu.HBM)
     inside = pl.BlockSpec(memory_space=pltpu.VMEM)

time: 56.5 us -> 56.5 us (level)
  no operation moved by 1% of the time
where the time goes in v5:
time: 56.5 us; the launch traced here: 56.4 us
  Pallas kernels  55.7 us (99%)
  between operations  0.65 us (1%)
    pallas_call x1, Pallas kernels, per_device(): pl.pallas_call(whole_step, name='whole_step', out_shape=tuple((pltpu.VMEM...  53.6 us
    pallas_call x1, Pallas kernels, per_device(): pl.pallas_call(write_out, name='write_out', out_shape=tuple((jax.ShapeDty...  2.14 us

profile of v5, /device:TPU:1, one launch (start us, length us, event | category | flops | bytes accessed | tf_op | source)
XLA Modules:
  0.0 56.4 jit_solution(11245821569819257588)
XLA Ops:
  0.6 53.6 %whole_step.1 = (f32[64,128]{1,0:T(8,128)S(1)}, f32[64,2,64,64]{3,2,1,0:T(8,128)S(1)}, bf16[64,128]{1,0:T(8,128)(2,1)S(1)}, bf16[64,128]{1,0:T(8,128)(2,1)S(1)}, bf16[64,128]{1,0:T(8,128)(2,1)S(1)}) custom-call(s32[1,64]{1,0:T(1,128)} %bitcast.19, bf16[2048,8,128]{2,1,0:T(8,128)(2,1)} %bitcast.17, bf16[64,128]{1,0:T(8,128)(2,1)} %prior_rec.1, ...), custom_call_target="tpu_custom_call" | custom-call | tf_op jit(solution)/shard_map/whole_step/pallas_call | solution.py:541
  54.2 2.1 %write_out.1 = (f32[64,128]{1,0:T(8,128)}, f32[64,2,64,64]{3,2,1,0:T(8,128)}, bf16[64,128]{1,0:T(8,128)(2,1)}, bf16[64,128]{1,0:T(8,128)(2,1)}, bf16[64,128]{1,0:T(8,128)(2,1)}) custom-call(f32[64,128]{1,0:T(8,128)S(1)} %get-tuple-element.10.refs_0_, f32[64,2,64,64]{3,2,1,0:T(8,128)S(1)} %get-tuple-element.11.refs_1_, ...), custom_call_target="tpu_custom_call" | custom-call | tf_op jit(solution)/shard_map/write_out/pallas_call | solution.py:552

commit v6 on v5

--- a/solution.py
+++ b/solution.py
@@ -191,7 +191,7 @@
     for i in range(ND):
         s = (d + (2, 1, 3, 0)[i]) % ND
 
-        @pl.loop(0, 8, unroll=4)
+        @pl.loop(0, 8, unroll=8)
         def _(g, s=s, i=i):
             block = jnp.zeros((8, 128), F32)
             for u in range(8):
@@ -237,7 +237,7 @@
         acc = gather_pass_on(buf, sem, got, p, add, (zero, zero))
         gather_end(buf, sem, got, p)
         acc = add(1 - p, q, acc)
-        acc = lax.fori_loop(0, NQ, lambda t, acc: add(p, t, acc), acc, unroll=4)
+        acc = lax.fori_loop(0, NQ, lambda t, acc: add(p, t, acc), acc, unroll=8)
         return mean_and_scale(pivot, acc)
 
     mean1, inv1 = gathered_norm(ebuf, esem, egot, 1 - c)
@@ -251,7 +251,7 @@
                 acc = body(cc, t, acc)
             return acc
 
-        return lax.fori_loop(0, NQ, step, init)
+        return lax.fori_loop(0, NQ, step, init, unroll=4)
 
     own_p = params(c, q)
     own_res = (ebuf[c, q].astype(F32) - mean1) * inv1 * own_p[0:1] + own_p[1:2]

time: 56.5 us -> 56.2 us (level)
  no operation moved by 1% of the time
where the time goes in v6:
time: 56.2 us; the launch traced here: 56.1 us
  Pallas kernels  55.5 us (99%)
  between operations  0.65 us (1%)
    pallas_call x1, Pallas kernels, per_device(): pl.pallas_call(whole_step, name='whole_step', out_shape=tuple((pltpu.VMEM...  53.3 us
    pallas_call x1, Pallas kernels, per_device(): pl.pallas_call(write_out, name='write_out', out_shape=tuple((jax.ShapeDty...  2.14 us

profile of v6, /device:TPU:1, one launch (start us, length us, event | category | flops | bytes accessed | tf_op | source)
XLA Modules:
  0.0 56.1 jit_solution(11047825583216579767)
XLA Ops:
  0.6 53.3 %whole_step.1 = (f32[64,128]{1,0:T(8,128)S(1)}, f32[64,2,64,64]{3,2,1,0:T(8,128)S(1)}, bf16[64,128]{1,0:T(8,128)(2,1)S(1)}, bf16[64,128]{1,0:T(8,128)(2,1)S(1)}, bf16[64,128]{1,0:T(8,128)(2,1)S(1)}) custom-call(s32[1,64]{1,0:T(1,128)} %bitcast.19, bf16[2048,8,128]{2,1,0:T(8,128)(2,1)} %bitcast.17, bf16[64,128]{1,0:T(8,128)(2,1)} %prior_rec.1, ...), custom_call_target="tpu_custom_call" | custom-call | tf_op jit(solution)/shard_map/whole_step/pallas_call | solution.py:541
  54.0 2.1 %write_out.1 = (f32[64,128]{1,0:T(8,128)}, f32[64,2,64,64]{3,2,1,0:T(8,128)}, bf16[64,128]{1,0:T(8,128)(2,1)}, bf16[64,128]{1,0:T(8,128)(2,1)}, bf16[64,128]{1,0:T(8,128)(2,1)}) custom-call(f32[64,128]{1,0:T(8,128)S(1)} %get-tuple-element.10.refs_0_, f32[64,2,64,64]{3,2,1,0:T(8,128)S(1)} %get-tuple-element.11.refs_1_, ...), custom_call_target="tpu_custom_call" | custom-call | tf_op jit(solution)/shard_map/write_out/pallas_call | solution.py:552
